TPU v7x, 128 devices: a whole 4x4x4 slice. The times are simulated.
128 devices in a mesh: blk: 8 (over z, x_lo), head: 16 (over y, x_hi, core).
Axes of the slice: x: 4 (x_hi: 2, x_lo: 2; x = x_hi * 2 + x_lo), y: 4, z: 4, core: 2. Of those that a mesh axis runs over, the one named last changes fastest.
Arguments:
- latent: float32 [128, 512, 256], P('blk', 'head'), may hold values from -6 to 6
- local_gain: float32 [256], replicated, may hold values from 0.5 to 1.5
- local_project: float32 [256, 768], replicated, may hold values from -0.375 to 0.375
- local_output: float32 [256, 256], replicated, may hold values from -0.375 to 0.375
- local_scale: float32 [4], replicated, may hold values from 2 to 500
- merge_first: float32 [1024, 384], replicated, may hold values from -0.1875 to 0.1875
- merge_second: float32 [1536, 512], replicated, may hold values from -0.15625 to 0.15625
- global_gain: float32 [512], replicated, may hold values from 0.5 to 1.5
- global_project: float32 [512, 1536], replicated, may hold values from -0.25 to 0.25
- global_output: float32 [512, 512], replicated, may hold values from -0.25 to 0.25
- global_scale: float32 [8], replicated, may hold values from 2 to 500
- split_second: float32 [512, 1536], replicated, may hold values from -0.25 to 0.25
- split_first: float32 [384, 1024], replicated, may hold values from -0.3125 to 0.3125
Outputs:
- refined: float32 [128, 512, 256], P('blk', 'head')
All inputs are finite; a program needn't handle non-finite values.
Results may differ from a plain program's by a relative error of at most 0.0003.
Values sent between devices are 32-bit elements; how exact they have to be, the bound alone decides.
No kernel may reach another device: no remote copies, remote signals or barrier semaphores. Data moves between devices by JAX's collectives and lax.ppermute only.
A program may use at most 128 MiB of HBM per device.

v0:
```python
import jax
import jax.numpy as jnp
from jax import lax
from jax.experimental import pallas as pl
from jax.experimental.pallas import tpu as pltpu
from jax.sharding import Mesh, PartitionSpec as P

C0 = 256
CM = 384
CG = 512
HEADS0 = 4
HEADS_G = 8
HEAD = 64
ROWS = 16
COLS = 32
PAD_ROWS = ROWS + 6
PAD_COLS = 40
BLOCK = 4
KEYS = (BLOCK + 6) * PAD_COLS
EPSILON = 1e-06
FLOOR_VALUE = 0.5
NEG = -1e30
HIGH = lax.Precision.HIGH
ZX = ("z", "xh", "xl")
YC = ("y", "c")
CLASSES = [(a1, b1, a2, b2) for a1 in (0, 1) for b1 in (0, 1) for a2 in (0, 1) for b2 in (0, 1)]


def mm(a, b):
    return jnp.dot(a, b, precision=HIGH, preferred_element_type=jnp.float32)


def mm_t(a, b):
    return lax.dot_general(
        a, b, (((1,), (1,)), ((), ())), precision=HIGH, preferred_element_type=jnp.float32
    )


def iota(shape, dim):
    return lax.broadcasted_iota(jnp.int32, shape, dim)


def head_mean(x):
    n = x.shape[1]
    same = iota((n, n), 0) // HEAD == iota((n, n), 1) // HEAD
    return mm(x * x, jnp.where(same, 1.0 / HEAD, 0.0))


def rms(x, gain):
    return x * lax.rsqrt(jnp.mean(x * x, axis=-1, keepdims=True) + EPSILON) * gain


def local_kernel(
    where_ref, x_ref, top_ref, bot_ref, left_ref, right_ref, tl_ref, tr_ref, bl_ref, br_ref,
    gain_ref, wp_ref, wo_ref, scale_ref, m1_ref, m2_ref, ggain_ref, wq_ref, gscale_ref,
    l0_ref, l1_ref, l2_ref, nx_ref, q_ref,
    pad, kk, vv, xq, qq, mask, lzero, spread,
):
    pad[3:19, 0:32, :] = x_ref[...]
    pad[0:3, 0:32, :] = top_ref[...]
    pad[19:22, 0:32, :] = bot_ref[...]
    pad[:, 32:40, :] = jnp.zeros((PAD_ROWS, 8, C0), jnp.float32)
    pad[3:19, 32:35, :] = right_ref[...]
    pad[3:19, 35:38, :] = left_ref[...]
    pad[0:3, 32:35, :] = tr_ref[...]
    pad[0:3, 35:38, :] = tl_ref[...]
    pad[19:22, 32:35, :] = br_ref[...]
    pad[19:22, 35:38, :] = bl_ref[...]
    gain = gain_ref[...]
    normed = rms(pad[...].reshape(PAD_ROWS * PAD_COLS, C0), gain)
    keys = mm(normed, wp_ref[:, C0 : 2 * C0])
    kk[...] = keys * lax.rsqrt(head_mean(keys) + EPSILON)
    vv[...] = mm(normed, wp_ref[:, 2 * C0 :])
    for half in range(2):
        spread[half] = x_ref[:, :, half * 128 : half * 128 + 128].reshape(512, 128)
    for t in range(ROWS // BLOCK):
        for n, (a1, b1, a2, b2) in enumerate(CLASSES):
            start = (BLOCK * t + 2 * a2 + a1) * COLS + 2 * b2 + b1
            for half in range(2):
                piece = spread[half, pl.ds(start, 8, stride=4), :]
                xq[t * 128 + n * 8 : t * 128 + n * 8 + 8, half * 128 : half * 128 + 128] = piece
    queries = mm(rms(xq[...], gain), wp_ref[:, :C0])
    qq[...] = queries * lax.rsqrt(head_mean(queries) + EPSILON) * scale_ref[...]

    qi = iota((128, KEYS), 0)
    ki = iota((128, KEYS), 1)
    cls = qi // 8
    q_row = 2 * ((cls // 2) % 2) + cls // 8
    q_col = 4 * (qi % 8) + 2 * (cls % 2) + (cls // 4) % 2
    slot = ki % PAD_COLS
    k_row = ki // PAD_COLS - 3
    k_col = jnp.where(slot < 35, slot, slot - 38)
    first_row = where_ref[0]
    first_col = where_ref[1]
    near = (
        (jnp.abs(k_row - q_row) <= 3)
        & (jnp.abs(k_col - q_col) <= 3)
        & (slot < 38)
        & (k_col + first_col >= 0)
        & (k_col + first_col < 512)
    )
    mask[...] = jnp.where(near, 0.0, NEG)
    lane_head = iota((128, C0), 1) // HEAD
    key_row = iota((1, KEYS), 1) // PAD_COLS - 3

    def block(t, carry):
        row = key_row + (first_row + t * BLOCK)
        bias = mask[...] + jnp.where((row >= 0) & (row < 128), 0.0, NEG)
        start = pl.multiple_of(t * (BLOCK * PAD_COLS), 8)
        k_now = kk[pl.ds(start, KEYS), :]
        v_now = vv[pl.ds(start, KEYS), :]
        q_start = pl.multiple_of(t * 128, 128)
        q_now = qq[pl.ds(q_start, 128), :]
        stacked = jnp.concatenate(
            [jnp.where(lane_head == h, q_now, 0.0) for h in range(HEADS0)], axis=0
        )
        scores = mm_t(stacked, k_now)
        weights = []
        sums = []
        for h in range(HEADS0):
            s = scores[h * 128 : (h + 1) * 128] + bias
            p = jnp.exp(s - jnp.max(s, axis=1, keepdims=True))
            weights.append(p)
            sums.append(jnp.sum(p, axis=1, keepdims=True))
        mixed = mm(jnp.concatenate(weights, axis=0), v_now)
        attended = jnp.zeros((128, C0), jnp.float32)
        for h in range(HEADS0):
            part = mixed[h * 128 : (h + 1) * 128] / sums[h]
            attended = jnp.where(lane_head == h, part, attended)
        level = xq[pl.ds(q_start, 128), :] + mm(attended, wo_ref[...])
        for n in range(16):
            at = pl.multiple_of(n * 32 + t * 8, 8)
            lzero[pl.ds(at, 8), :] = level[n * 8 : (n + 1) * 8]
        return carry

    lax.fori_loop(0, ROWS // BLOCK, block, 0)
    l0_ref[...] = lzero[...]
    one = mm(lzero[0:128, :], m1_ref[0:C0, :])
    for n in range(1, 4):
        one = one + mm(lzero[n * 128 : (n + 1) * 128, :], m1_ref[n * C0 : (n + 1) * C0, :])
    l1_ref[...] = one
    two = mm(one[0:32], m2_ref[0:CM, :])
    for n in range(1, 4):
        two = two + mm(one[n * 32 : (n + 1) * 32], m2_ref[n * CM : (n + 1) * CM, :])
    l2_ref[...] = two
    normed_two = rms(two, ggain_ref[...])
    q = mm(normed_two, wq_ref[...])
    q = q * lax.rsqrt(jnp.maximum(head_mean(q), FLOOR_VALUE)) * gscale_ref[...]
    for n in range(16):
        nx_ref[n] = normed_two
    for n in range(8):
        q_ref[n] = q


def attention_kernel(x_ref, q_ref, wk_ref, wv_ref, out_ref, kk, vv):
    x = x_ref[...].reshape(512, CG)
    keys = mm(x, wk_ref[...])
    kk[...] = keys * lax.rsqrt(jnp.maximum(head_mean(keys), FLOOR_VALUE))
    vv[...] = mm(x, wv_ref[...])
    lane_head = iota((256, 256), 1) // HEAD
    lane = iota((256, 128), 1)
    extra = jnp.zeros((256, 128), jnp.float32)
    q = q_ref[...].reshape(256, CG)
    for g in range(2):
        cols = slice(g * 256, (g + 1) * 256)
        k_now = kk[:, cols]
        v_now = vv[:, cols]
        acc = jnp.zeros((256, 256), jnp.float32)
        for h in range(4):
            s = mm_t(jnp.where(lane_head == h, q[:, cols], 0.0), k_now)
            m = jnp.max(s, axis=1, keepdims=True)
            p = jnp.exp(s - m)
            acc = jnp.where(lane_head == h, mm(p, v_now), acc)
            extra = jnp.where(lane == g * 4 + h, m, extra)
            extra = jnp.where(lane == 8 + g * 4 + h, jnp.sum(p, axis=1, keepdims=True), extra)
        out_ref[:, :, cols] = acc.reshape(8, 32, 256)
    out_ref[:, :, CG:] = extra.reshape(8, 32, 128)


def tail_kernel(part_ref, l0_ref, l1_ref, l2_ref, go_ref, s2_ref, s1_ref, out_ref, spread):
    best = part_ref[0, :, CG:]
    for n in range(1, 8):
        best = jnp.maximum(best, part_ref[n, :, CG:])
    row = iota((128, CG), 0)
    head = iota((128, CG), 1) // HEAD
    pick_weight = jnp.where(row == head, 1.0, 0.0)
    lane = iota((32, 128), 1)
    total = jnp.zeros((32, CG), jnp.float32)
    sums = jnp.zeros((32, 128), jnp.float32)
    for n in range(8):
        extra = part_ref[n, :, CG:]
        w = jnp.where(lane < 8, jnp.exp(extra - best), 0.0)
        sums = sums + w * pltpu.roll(extra, 120, 1)
        factor = jnp.dot(
            w, pick_weight, precision=lax.Precision.HIGHEST, preferred_element_type=jnp.float32
        )
        total = total + factor * part_ref[n, :, 0:CG]
    inverse = jnp.where(lane < 8, 1.0 / jnp.where(lane < 8, sums, 1.0), 0.0)
    factor = jnp.dot(
        inverse, pick_weight, precision=lax.Precision.HIGHEST, preferred_element_type=jnp.float32
    )
    mixed = l2_ref[...] + mm(total * factor, go_ref[...])
    second = mm(mixed, s2_ref[...])
    up = jnp.concatenate(
        [l1_ref[n * 32 : (n + 1) * 32, :] + second[:, n * CM : (n + 1) * CM] for n in range(4)],
        axis=0,
    )
    first = mm(up, s1_ref[...])
    for n, (a1, b1, a2, b2) in enumerate(CLASSES):
        c1 = a1 * 2 + b1
        c2 = a2 * 2 + b2
        piece = l0_ref[n * 32 : (n + 1) * 32, :] + first[
            c2 * 32 : (c2 + 1) * 32, c1 * C0 : (c1 + 1) * C0
        ]
        for i in range(4):
            start = (BLOCK * i + 2 * a2 + a1) * COLS + 2 * b2 + b1
            for half in range(2):
                spread[half, pl.ds(start, 8, stride=4), :] = piece[
                    i * 8 : (i + 1) * 8, half * 128 : half * 128 + 128
                ]
    for half in range(2):
        out_ref[:, :, half * 128 : half * 128 + 128] = spread[half].reshape(ROWS, COLS, 128)


def f32(*shape):
    return jax.ShapeDtypeStruct(shape, jnp.float32)


def shift(n, step):
    return [(i, i + step) for i in range(n) if 0 <= i + step < n]


def shards(
    latent, local_gain, local_project, local_output, local_scale, merge_first, merge_second,
    global_gain, global_project, global_output, global_scale, split_second, split_first,
):
    row_axis = ("z", "xl")
    col_axis = ("y", "xh", "c")
    both = row_axis + col_axis

    def moved(value, dr, dc):
        if dc == 0:
            return lax.ppermute(value, row_axis, shift(8, dr))
        if dr == 0:
            return lax.ppermute(value, col_axis, shift(16, dc))
        pairs = [(i * 16 + k, j * 16 + m) for i, j in shift(8, dr) for k, m in shift(16, dc)]
        return lax.ppermute(value, both, pairs)

    top = moved(latent[13:], 1, 0)
    bot = moved(latent[:3], -1, 0)
    left = moved(latent[:, 29:], 0, 1)
    right = moved(latent[:, :3], 0, -1)
    tl = moved(latent[13:, 29:], 1, 1)
    tr = moved(latent[13:, :3], 1, -1)
    bl = moved(latent[:3, 29:], -1, 1)
    br = moved(latent[:3, :3], -1, -1)
    split = global_project.reshape(CG, HEADS_G, 3, HEAD)
    wq = split[:, :, 0].reshape(CG, CG)
    wk = split[:, :, 1].reshape(CG, CG)
    wv = split[:, :, 2].reshape(CG, CG)
    where = jnp.stack([lax.axis_index(row_axis) * ROWS, lax.axis_index(col_axis) * COLS])
    scale0 = jnp.repeat(local_scale / HEAD, HEAD)[None]
    scale_g = jnp.repeat(global_scale / HEAD, HEAD)[None]
    vmem = pl.BlockSpec(memory_space=pltpu.VMEM)
    smem = pl.BlockSpec(memory_space=pltpu.SMEM)
    l0, l1, l2, nx, q = pl.pallas_call(
        local_kernel,
        out_shape=(f32(512, C0), f32(128, CM), f32(32, CG), f32(16, 32, CG), f32(8, 32, CG)),
        in_specs=[smem] + [vmem] * 18,
        out_specs=[vmem] * 5,
        scratch_shapes=[
            pltpu.VMEM((PAD_ROWS, PAD_COLS, C0), jnp.float32),
            pltpu.VMEM((PAD_ROWS * PAD_COLS, C0), jnp.float32),
            pltpu.VMEM((PAD_ROWS * PAD_COLS, C0), jnp.float32),
            pltpu.VMEM((512, C0), jnp.float32),
            pltpu.VMEM((512, C0), jnp.float32),
            pltpu.VMEM((128, KEYS), jnp.float32),
            pltpu.VMEM((512, C0), jnp.float32),
            pltpu.VMEM((2, 512, 128), jnp.float32),
        ],
        name="local",
    )(
        where, latent, top, bot, left, right, tl, tr, bl, br,
        local_gain[None], local_project, local_output, scale0, merge_first, merge_second,
        global_gain[None], wq, scale_g,
    )
    keys_from = lax.all_to_all(nx, ZX, 0, 0, tiled=True)
    queries_from = lax.all_to_all(q, YC, 0, 0, tiled=True)
    part = pl.pallas_call(
        attention_kernel,
        out_shape=f32(8, 32, CG + 128),
        in_specs=[vmem] * 4,
        out_specs=vmem,
        scratch_shapes=[pltpu.VMEM((512, CG), jnp.float32), pltpu.VMEM((512, CG), jnp.float32)],
        name="attend",
    )(keys_from, queries_from, wk, wv)
    part = lax.all_to_all(part, YC, 0, 0, tiled=True)
    return pl.pallas_call(
        tail_kernel,
        out_shape=f32(ROWS, COLS, C0),
        in_specs=[vmem] * 7,
        out_specs=vmem,
        scratch_shapes=[pltpu.VMEM((2, 512, 128), jnp.float32)],
        name="tail",
    )(part, l0, l1, l2, global_output, split_second, split_first)


def solution(mesh):
    fine = Mesh(mesh.devices.reshape(4, 2, 4, 2, 2), ("z", "xl", "y", "xh", "c"))
    tile = P(("z", "xl"), ("y", "xh", "c"), None)
    return jax.shard_map(
        shards, mesh=fine, in_specs=(tile,) + (P(),) * 12, out_specs=tile, check_vma=False
    )
```

profile of v0, /device:TPU:1, one launch (start us, length us, event | category | flops | bytes accessed | tf_op | source)
XLA Modules:
  0.0 134.5 jit_solution(8363427336083082450)
XLA Ops:
  0.0 1.4 %fusion.1 = (f32[3,3,256]{2,1,0:T(4,128)}, f32[3,3,256]{2,1,0:T(4,128)}, f32[3,3,256]{2,1,0:T(4,128)}, f32[3,3,256]{2,1,0:T(4,128)}) fusion(f32[16,32,256]{2,1,0:T(8,128)} %x_ref.1), kind=kLoop, calls=%fused_computation.4 | loop fusion | bytes 73728 | tf_op jit(solution)/shard_map/slice | solution.py:256
  1.4 5.7 %collective-permute-start.4 = (f32[3,3,256]{2,1,0:T(4,128)}, f32[3,3,256]{2,1,0:T(4,128)S(1)}, u32[]{:S(2)}, u32[]{:S(2)}) collective-permute-start(f32[3,3,256]{2,1,0:T(4,128)} %get-tuple-element.21), channel_id=1, source_target_pairs={{0,17},{1,18},{2,19},{3,20},{4,21},{5,22},{6,23},{7,24},{8,25},{9,... | collective-permute-start | bytes 27656 | tf_op jit(solution)/shard_map/ppermute | solution.py:247
  7.2 2.0 %collective-permute-start.5 = (f32[3,3,256]{2,1,0:T(4,128)}, f32[3,3,256]{2,1,0:T(4,128)S(1)}, u32[]{:S(2)}, u32[]{:S(2)}) collective-permute-start(f32[3,3,256]{2,1,0:T(4,128)} %get-tuple-element.20), channel_id=1, source_target_pairs={{1,16},{2,17},{3,18},{4,19},{5,20},{6,21},{7,22},{8,23},{9,24},{10... | collective-permute-start | bytes 27656 | tf_op jit(solution)/shard_map/ppermute | solution.py:247
  9.1 1.3 collective-permute-start.6
  10.4 1.3 collective-permute-start.7
  11.7 1.0 fusion.3
  12.7 6.1 %collective-permute-start = (f32[3,32,256]{2,1,0:T(8,128)S(1)}, f32[3,32,256]{2,1,0:T(8,128)S(1)}, u32[]{:S(2)}, u32[]{:S(2)}) collective-permute-start(f32[3,32,256]{2,1,0:T(8,128)S(1)} %get-tuple-element.25), channel_id=1, source_target_pairs={{0,16},{16,32},{32,48},{48,64},{64,80},{80,96},{96,112},{1,17},{17... | collective-permute-start | bytes 294920 | tf_op jit(solution)/shard_map/ppermute | solution.py:243
  18.9 1.6 %fusion.2 = (f32[16,3,256]{2,1,0:T(4,128)S(1)}, f32[16,3,256]{2,1,0:T(4,128)}) fusion(f32[16,32,256]{2,1,0:T(8,128)} %x_ref.1), kind=kLoop, calls=%fused_computation.5 | loop fusion | bytes 196608 | tf_op jit(solution)/shard_map/slice | solution.py:252
  20.5 2.4 %copy.17 = f32[512,1536]{0,1:T(8,128)S(1)} copy(f32[512,1536]{1,0:T(8,128)} %param.21) | data formatting | bytes 6291456 | tf_op args[8]
  22.9 1.8 %fusion = (f32[512,8,1,64]{0,3,2,1:T(8,128)}, f32[512,8,1,64]{0,3,2,1:T(8,128)}, f32[512,8,1,64]{0,3,2,1:T(8,128)}) fusion(f32[512,8,3,64]{0,3,2,1:T(8,128)S(1)} %bitcast.8), kind=kLoop, calls=%fused_computation.3 | loop fusion | bytes 6291456 | tf_op jit(solution)/shard_map/slice | solution.py:260
  24.7 1.3 collective-permute-start.1
  26.0 4.7 %collective-permute-start.2 = (f32[16,3,256]{2,1,0:T(4,128)}, f32[16,3,256]{2,1,0:T(4,128)S(1)}, u32[]{:S(2)}, u32[]{:S(2)}) collective-permute-start(f32[16,3,256]{2,1,0:T(4,128)} %get-tuple-element.23), channel_id=1, source_target_pairs={{0,1},{1,2},{2,3},{3,4},{4,5},{5,6},{6,7},{7,8},{8,9},{9,10},{10,1... | collective-permute-start | bytes 147464 | tf_op jit(solution)/shard_map/ppermute | solution.py:245
  30.7 1.9 %collective-permute-start.3 = (f32[16,3,256]{2,1,0:T(4,128)S(1)}, f32[16,3,256]{2,1,0:T(4,128)S(1)}, u32[]{:S(2)}, u32[]{:S(2)}) collective-permute-start(f32[16,3,256]{2,1,0:T(4,128)S(1)} %get-tuple-element.22), channel_id=1, source_target_pairs={{1,0},{2,1},{3,2},{4,3},{5,4},{6,5},{7,6},{8,7},{9,8},{10,9},{11,1... | collective-permute-start | bytes 147464 | tf_op jit(solution)/shard_map/ppermute | solution.py:245
  32.6 0.6 pad_add_fusion.where_ref
  33.3 2.5 %copy.18.wq_ref = f32[512,512]{1,0:T(8,128)} copy(f32[512,512]{0,1:T(8,128)} %bitcast.11) | data formatting | bytes 2097152 | tf_op jit(solution)/shard_map/reshape;squeeze | solution.py:258
  35.8 0.1 broadcast_in_dim.15
  35.9 0.7 broadcast_in_dim_reshape.7.gscale_ref
  36.5 0.1 broadcast_in_dim.13
  36.6 0.7 broadcast_in_dim_reshape.6.scale_ref
  37.3 0.5 collective-permute-done.3.right_ref
  37.9 0.5 copy-done.6
  38.5 0.1 copy-done.4
  38.5 17.7 %local.1 = (f32[512,256]{1,0:T(8,128)}, f32[128,384]{1,0:T(8,128)}, f32[32,512]{1,0:T(8,128)}, f32[16,32,512]{2,1,0:T(8,128)}, f32[8,32,512]{2,1,0:T(8,128)}) custom-call(s32[2]{0:T(128)} %pad_add_fusion.where_ref, f32[16,32,256]{2,1,0:T(8,128)} %x_ref.1, f32[3,32,256]{2,1,0:T(8,128)} %copy-done.3, f32[3,32,256]{2,1,0:T(8,128)} %copy-done.4, ...), custom_call_target="tpu_custom_call" | custom-call | tf_op jit(solution)/shard_map/local/pallas_call | solution.py:266
  56.2 15.7 %all_to_all.15.q_ref = f32[8,32,512]{2,1,0:T(8,128)} all-to-all(f32[8,32,512]{2,1,0:T(8,128)} %get-tuple-element.11), channel_id=1, replica_groups=mesh['z'=4,'xl'=2,'y'=4,'xh'=2,'c'=2] {'y','c'}, dimensions={0} | all-to-all | bytes 1048576 | tf_op jit(solution)/shard_map/all_to_all | solution.py:288
  71.9 11.8 %all-to-all-start = ((f32[16,32,512]{2,1,0:T(8,128)}), f32[16,32,512]{2,1,0:T(8,128)S(1)}, u32[]{:S(2)}, u32[]{:S(2)}) async-start(f32[16,32,512]{2,1,0:T(8,128)} %get-tuple-element.10), calls=%async_computation | async-start | bytes 2097152 | tf_op jit(solution)/shard_map/all_to_all | solution.py:287
  83.7 1.3 copy.19.wk_ref
  85.0 1.3 %copy.20.wv_ref = f32[512,512]{1,0:T(8,128)} copy(f32[512,512]{0,1:T(8,128)S(1)} %bitcast.9) | data formatting | bytes 2097152 | tf_op jit(solution)/shard_map/reshape;squeeze | solution.py:260
  86.4 13.0 %all-to-all-done.x_ref = f32[16,32,512]{2,1,0:T(8,128)S(1)} async-done(((f32[16,32,512]{2,1,0:T(8,128)}), f32[16,32,512]{2,1,0:T(8,128)S(1)}, u32[]{:S(2)}, u32[]{:S(2)}) %all-to-all-start) | async-done | bytes 1048608 | tf_op jit(solution)/shard_map/all_to_all | solution.py:287
  99.4 1.0 copy-done.2
  100.4 9.5 %attend.1 = f32[8,32,640]{2,1,0:T(8,128)} custom-call(f32[16,32,512]{2,1,0:T(8,128)} %copy-done.2, f32[8,32,512]{2,1,0:T(8,128)} %all_to_all.15.q_ref, f32[512,512]{1,0:T(8,128)} %copy.19.wk_ref, f32[512,512]{1,0:T(8,128)} %copy.20.wv_ref), custom_call_target="tpu_custom_call" | custom-call | tf_op jit(solution)/shard_map/attend/pallas_call | solution.py:289
  109.9 18.0 %all_to_all.16.part_ref = f32[8,32,640]{2,1,0:T(8,128)} all-to-all(f32[8,32,640]{2,1,0:T(8,128)} %attend.1), channel_id=1, replica_groups=mesh['z'=4,'xl'=2,'y'=4,'xh'=2,'c'=2] {'y','c'}, dimensions={0} | all-to-all | bytes 1310720 | tf_op jit(solution)/shard_map/all_to_all | solution.py:297
  127.8 6.6 %tail.1 = f32[16,32,256]{2,1,0:T(8,128)} custom-call(f32[8,32,640]{2,1,0:T(8,128)} %all_to_all.16.part_ref, f32[512,256]{1,0:T(8,128)} %get-tuple-element.12.l0_ref, f32[128,384]{1,0:T(8,128)} %get-tuple-element.13.l1_ref, f32[32,512]{1,0:T(8,128)} %get-tuple-element.14.l2_ref, f32[512,512]{1,0:T(8,128)} %go_ref.1, f32[512,1536]{1,0:T(8,128)} %s2_ref.1, ...), custom_call_target="tpu_custom_call" | custom-call | tf_op jit(solution)/shard_map/tail/pallas_call | solution.py:298
  (32 shorter events, 0.2 us)
Async XLA Ops:
  1.4 23.3 %collective-permute-start.4 = (f32[3,3,256]{2,1,0:T(4,128)}, f32[3,3,256]{2,1,0:T(4,128)S(1)}, u32[]{:S(2)}, u32[]{:S(2)}) collective-permute-start(f32[3,3,256]{2,1,0:T(4,128)} %get-tuple-element.21), channel_id=1, source_target_pairs={{0,17},{1,18},{2,19},{3,20},{4,21},{5,22},{6,23},{7,24},{8,25},{9,... | collective-permute-start | bytes 27656 | tf_op jit(solution)/shard_map/ppermute | solution.py:247
  7.2 18.8 %collective-permute-start.5 = (f32[3,3,256]{2,1,0:T(4,128)}, f32[3,3,256]{2,1,0:T(4,128)S(1)}, u32[]{:S(2)}, u32[]{:S(2)}) collective-permute-start(f32[3,3,256]{2,1,0:T(4,128)} %get-tuple-element.20), channel_id=1, source_target_pairs={{1,16},{2,17},{3,18},{4,19},{5,20},{6,21},{7,22},{8,23},{9,24},{10... | collective-permute-start | bytes 27656 | tf_op jit(solution)/shard_map/ppermute | solution.py:247
  9.1 21.5 %collective-permute-start.6 = (f32[3,3,256]{2,1,0:T(4,128)}, f32[3,3,256]{2,1,0:T(4,128)S(1)}, u32[]{:S(2)}, u32[]{:S(2)}) collective-permute-start(f32[3,3,256]{2,1,0:T(4,128)} %get-tuple-element.19), channel_id=1, source_target_pairs={{16,1},{17,2},{18,3},{19,4},{20,5},{21,6},{22,7},{23,8},{24,9},{25... | collective-permute-start | bytes 27656 | tf_op jit(solution)/shard_map/ppermute | solution.py:247
  10.4 26.8 %collective-permute-start.7 = (f32[3,3,256]{2,1,0:T(4,128)}, f32[3,3,256]{2,1,0:T(4,128)S(1)}, u32[]{:S(2)}, u32[]{:S(2)}) collective-permute-start(f32[3,3,256]{2,1,0:T(4,128)} %get-tuple-element.18), channel_id=1, source_target_pairs={{17,0},{18,1},{19,2},{20,3},{21,4},{22,5},{23,6},{24,7},{25,8},{26... | collective-permute-start | bytes 27656 | tf_op jit(solution)/shard_map/ppermute | solution.py:247
  12.7 25.1 %collective-permute-start = (f32[3,32,256]{2,1,0:T(8,128)S(1)}, f32[3,32,256]{2,1,0:T(8,128)S(1)}, u32[]{:S(2)}, u32[]{:S(2)}) collective-permute-start(f32[3,32,256]{2,1,0:T(8,128)S(1)} %get-tuple-element.25), channel_id=1, source_target_pairs={{0,16},{16,32},{32,48},{48,64},{64,80},{80,96},{96,112},{1,17},{17... | collective-permute-start | bytes 294920 | tf_op jit(solution)/shard_map/ppermute | solution.py:243
  22.9 1.8 %copy-start.11 = (f32[8]{0:T(128)S(1)}, f32[8]{0:T(128)}, u32[]{:S(2)}) copy-start(f32[8]{0:T(128)} %param.23) | copy-start | bytes 100
  22.9 1.8 %copy-start.12 = (f32[4]{0:T(128)S(1)}, f32[4]{0:T(128)}, u32[]{:S(2)}) copy-start(f32[4]{0:T(128)} %param.17) | copy-start | bytes 52
  24.7 13.1 %copy-start.7 = (f32[3,3,256]{2,1,0:T(4,128)}, f32[3,3,256]{2,1,0:T(4,128)S(1)}, u32[]{:S(2)}) copy-start(f32[3,3,256]{2,1,0:T(4,128)S(1)} %collective-permute-done.4.tl_ref) | copy-start | bytes 27652
  24.7 13.1 %collective-permute-start.1 = (f32[3,32,256]{2,1,0:T(8,128)S(1)}, f32[3,32,256]{2,1,0:T(8,128)S(1)}, u32[]{:S(2)}, u32[]{:S(2)}) collective-permute-start(f32[3,32,256]{2,1,0:T(8,128)S(1)} %get-tuple-element.24), channel_id=1, source_target_pairs={{16,0},{32,16},{48,32},{64,48},{80,64},{96,80},{112,96},{17,1},{33... | collective-permute-start | bytes 294920 | tf_op jit(solution)/shard_map/ppermute | solution.py:243
  26.0 11.8 %copy-start.8 = (f32[3,3,256]{2,1,0:T(4,128)}, f32[3,3,256]{2,1,0:T(4,128)S(1)}, u32[]{:S(2)}) copy-start(f32[3,3,256]{2,1,0:T(4,128)S(1)} %collective-permute-done.5.tr_ref) | copy-start | bytes 27652
  26.0 11.3 %collective-permute-start.2 = (f32[16,3,256]{2,1,0:T(4,128)}, f32[16,3,256]{2,1,0:T(4,128)S(1)}, u32[]{:S(2)}, u32[]{:S(2)}) collective-permute-start(f32[16,3,256]{2,1,0:T(4,128)} %get-tuple-element.23), channel_id=1, source_target_pairs={{0,1},{1,2},{2,3},{3,4},{4,5},{5,6},{6,7},{7,8},{8,9},{9,10},{10,1... | collective-permute-start | bytes 147464 | tf_op jit(solution)/shard_map/ppermute | solution.py:245
  30.7 7.1 %copy-start.9 = (f32[3,3,256]{2,1,0:T(4,128)}, f32[3,3,256]{2,1,0:T(4,128)S(1)}, u32[]{:S(2)}) copy-start(f32[3,3,256]{2,1,0:T(4,128)S(1)} %collective-permute-done.6.bl_ref) | copy-start | bytes 27652
  30.7 7.1 %collective-permute-start.3 = (f32[16,3,256]{2,1,0:T(4,128)S(1)}, f32[16,3,256]{2,1,0:T(4,128)S(1)}, u32[]{:S(2)}, u32[]{:S(2)}) collective-permute-start(f32[16,3,256]{2,1,0:T(4,128)S(1)} %get-tuple-element.22), channel_id=1, source_target_pairs={{1,0},{2,1},{3,2},{4,3},{5,4},{6,5},{7,6},{8,7},{9,8},{10,9},{11,1... | collective-permute-start | bytes 147464 | tf_op jit(solution)/shard_map/ppermute | solution.py:245
  37.3 0.6 copy-start.10
  37.3 0.6 copy-start.5
  37.8 0.6 copy-start.6
  37.8 0.7 copy-start.3
  37.8 0.7 copy-start.4
  56.2 27.5 %copy-start.1 = (f32[512,8,1,64]{0,3,2,1:T(8,128)S(1)}, f32[512,8,1,64]{0,3,2,1:T(8,128)}, u32[]{:S(2)}) copy-start(f32[512,8,1,64]{0,3,2,1:T(8,128)} %get-tuple-element.16) | copy-start | bytes 3145732
  56.2 28.8 %copy-start = (f32[512,8,1,64]{0,3,2,1:T(8,128)S(1)}, f32[512,8,1,64]{0,3,2,1:T(8,128)}, u32[]{:S(2)}) copy-start(f32[512,8,1,64]{0,3,2,1:T(8,128)} %get-tuple-element.15) | copy-start | bytes 3145732
  71.9 27.5 %all-to-all-start = ((f32[16,32,512]{2,1,0:T(8,128)}), f32[16,32,512]{2,1,0:T(8,128)S(1)}, u32[]{:S(2)}, u32[]{:S(2)}) async-start(f32[16,32,512]{2,1,0:T(8,128)} %get-tuple-element.10), calls=%async_computation | async-start | bytes 2097152 | tf_op jit(solution)/shard_map/all_to_all | solution.py:287
  99.4 1.0 copy-start.2
where the time goes:
time: 135 us; the launch traced here: 134 us
  starting transfers between devices  36.1 us (27%)
  Pallas kernels  33.8 us (25%)
  blocking collectives  33.6 us (25%)
  local copies, waits for them, and re-layouts  16.5 us (12%)
  waiting for transfers between devices  13.5 us (10%)
    all_to_all x1, blocking collectives, shards(): part = lax.all_to_all(part, YC, 0, 0, tiled=True)  18 us
    pallas_call x1, Pallas kernels, shards(): pl.pallas_call(local_kernel, out_shape=(f32(512, C0), f32(128, CM), f32(3...  17.7 us
    all_to_all x1, blocking collectives, shards(): queries_from = lax.all_to_all(q, YC, 0, 0, tiled=True)  15.7 us
    all_to_all x1, waiting for transfers between devices, shards(): keys_from = lax.all_to_all(nx, ZX, 0, 0, tiled=True)  13 us
    all_to_all x1, starting transfers between devices, shards(): keys_from = lax.all_to_all(nx, ZX, 0, 0, tiled=True)  11.8 us
    ppermute x4, starting transfers between devices, moved(): return lax.ppermute(value, both, pairs)  10.3 us
    pallas_call x1, Pallas kernels, shards(): pl.pallas_call(attention_kernel, out_shape=f32(8, 32, CG + 128), in_specs...  9.46 us
    ppermute x2, starting transfers between devices, moved(): return lax.ppermute(value, row_axis, shift(8, dr))  7.43 us
  transfers between devices with their start and end apart: 9, of which 2 were waited for; matrix products, arithmetic and copies ran while one was open for 10% of the time, Pallas kernels for 0%

commit v1 on v0

v1 whole, which is shorter than its diff:
```python
import jax
import jax.numpy as jnp
from jax import lax
from jax.experimental import pallas as pl
from jax.experimental.pallas import tpu as pltpu
from jax.sharding import Mesh, PartitionSpec as P

C0 = 256
CM = 384
CG = 512
HEADS0 = 4
HEADS_G = 8
HEAD = 64
ROWS = 16
COLS = 32
HALF = 16
BLOCK = 4
WINDOW = BLOCK + 6
SLOTS = 24
KEYS = WINDOW * SLOTS
QUERIES = BLOCK * HALF
HEIGHT = 128
BREADTH = 512
EPSILON = 1e-06
FLOOR_VALUE = 0.5
NEG = -1e30
HIGH = lax.Precision.HIGH
HIGHEST = lax.Precision.HIGHEST
BF = jnp.bfloat16
F32 = jnp.float32
ROW_AXIS = ("z", "xl")
COL_AXIS = ("y", "xh", "c")
ZX = ("z", "xh", "xl")
TURNS = (1, 3, 2)
CLASSES = [(a1, b1, a2, b2) for a1 in (0, 1) for b1 in (0, 1) for a2 in (0, 1) for b2 in (0, 1)]


def mm(a, b, precision=HIGH):
    return jnp.dot(a, b, precision=precision, preferred_element_type=F32)


def iota(shape, dim):
    return lax.broadcasted_iota(jnp.int32, shape, dim)


def parts(x):
    hi = x.astype(BF)
    return hi, (x - hi.astype(F32)).astype(BF)


def head_mean(x):
    n = x.shape[1]
    same = iota((n, n), 0) // HEAD == iota((n, n), 1) // HEAD
    weight = jnp.where(same, 1.0 / HEAD, 0.0).astype(BF)
    hi, lo = parts(x * x)
    return jnp.dot(hi, weight, preferred_element_type=F32) + jnp.dot(
        lo, weight, preferred_element_type=F32
    )


def rms(x, gain):
    return x * lax.rsqrt(jnp.mean(x * x, axis=-1, keepdims=True) + EPSILON) * gain


def unit(x):
    return x * lax.rsqrt(head_mean(x) + EPSILON)


def floored(x):
    return x * lax.rsqrt(jnp.maximum(head_mean(x), FLOOR_VALUE))


def lanes_of(ref, heads):
    lane = iota((1, heads * HEAD), 1) // HEAD
    out = jnp.zeros((1, heads * HEAD), F32)
    for h in range(heads):
        out = jnp.where(lane == h, ref[h] * (1.0 / HEAD), out)
    return out


def two_halves(x):
    hi = x.astype(BF).astype(F32)
    lo = x - hi
    return hi, lo, pltpu.roll(hi, HEAD, 1), pltpu.roll(lo, HEAD, 1)


def pair_keys(tile, first):
    hi, lo, hi_r, lo_r = two_halves(tile)
    a = jnp.concatenate([jnp.where(first, hi, hi_r), jnp.where(first, lo, lo_r)], axis=1)
    b = jnp.concatenate([jnp.where(first, hi_r, hi), jnp.where(first, lo_r, lo)], axis=1)
    return a.astype(BF), b.astype(BF)


def pair_queries(tile, first):
    hi = tile.astype(BF).astype(F32)
    lo = pltpu.roll(tile - hi, HEAD, 1)
    a = jnp.where(first, hi, lo).astype(BF)
    b = jnp.where(first, lo, hi).astype(BF)
    return jnp.concatenate([a, a], axis=1), jnp.concatenate([b, b], axis=1)


def pair_values(tile, first):
    hi = tile.astype(BF).astype(F32)
    lo = pltpu.roll(tile - hi, HEAD, 1)
    return jnp.where(first, hi, lo).astype(BF), jnp.where(first, lo, hi).astype(BF)


def scored(q, k):
    return lax.dot_general(q, k, (((1,), (1,)), ((), ())), preferred_element_type=F32)


def mixed_values(p, v):
    n = p.shape[0]
    hi, lo = parts(p)
    r = jnp.dot(jnp.concatenate([hi, lo], axis=0), v, preferred_element_type=F32)
    r = r[:n] + r[n:]
    return r + pltpu.roll(r, HEAD, 1)


def edge_kernel(x_ref, first_ref, last_ref):
    first_ref[...] = x_ref[:, 0:3, :]
    last_ref[...] = x_ref[:, COLS - 3 : COLS, :]


def row_kernel(x_ref, left_ref, right_ref, up_ref, down_ref):
    for ref, at in ((up_ref, 0), (down_ref, ROWS - 3)):
        ref[:, 0:COLS, :] = x_ref[at : at + 3]
        ref[:, COLS : COLS + 8, :] = jnp.zeros((3, 8, C0), F32)
        ref[:, COLS : COLS + 3, :] = right_ref[at : at + 3]
        ref[:, COLS + 3 : COLS + 6, :] = left_ref[at : at + 3]


def own_kernel(
    x_ref, gain_hbm, wp_hbm, scale_hbm, q_ref, k_ref, v_ref, gain, weight, scale, sems
):
    gain_in = pltpu.make_async_copy(gain_hbm, gain, sems.at[0])
    scale_in = pltpu.make_async_copy(scale_hbm, scale, sems.at[1])
    weight_in = pltpu.make_async_copy(wp_hbm, weight, sems.at[2])
    gain_in.start()
    weight_in.start()
    scale_in.start()
    gain_in.wait()
    normed = rms(x_ref[...].reshape(ROWS * COLS, C0), gain[...])
    weight_in.wait()
    q = mm(normed, weight[:, 0:C0], HIGHEST)
    scale_in.wait()
    q_ref[...] = unit(q) * lanes_of(scale, HEADS0)
    k = mm(normed, weight[:, C0 : 2 * C0], HIGHEST)
    k_ref[...] = unit(k).reshape(ROWS, COLS, C0)
    v_ref[...] = mm(normed, weight[:, 2 * C0 :]).reshape(ROWS, COLS, C0)


def keys_values(raw, gain_ref, wp_ref):
    normed = rms(raw, gain_ref[...])
    k = unit(mm(normed, wp_ref[:, C0 : 2 * C0], HIGHEST))
    return k, mm(normed, wp_ref[:, 2 * C0 :])


def windowed(own, side):
    sub = iota((1, 8, 1), 1)
    left = jnp.concatenate(
        [own[:, 0:16], jnp.where(sub < 3, own[:, 16:24], side)], axis=1
    )
    right = jnp.concatenate(
        [own[:, 16:32], jnp.where(sub >= 5, own[:, 8:16], side)], axis=1
    )
    return left, right


def near_masks(first_col):
    qi = iota((QUERIES, KEYS), 0)
    ki = iota((QUERIES, KEYS), 1)
    slot = ki % SLOTS
    row_near = jnp.abs(ki // SLOTS - 3 - qi // HALF) <= 3
    out = []
    for half in range(2):
        if half == 0:
            col = jnp.where(slot < 19, slot, slot - 22)
            real = slot < 22
        else:
            col = jnp.where(slot < 19, slot + 16, slot - 8)
            real = (slot < 19) | (slot >= 21)
        near = jnp.abs(col - (qi % HALF + half * HALF)) <= 3
        place = col + first_col
        inside = (place >= 0) & (place < BREADTH)
        out.append(jnp.where(row_near & near & real & inside, 0.0, NEG))
    return out


def window_block(q, k, v, bias, first):
    tiles = []
    for m in range(2):
        cols = slice(m * 128, (m + 1) * 128)
        queries = pair_queries(q[:, cols], first)
        keys = pair_keys(k[:, cols], first)
        values = pair_values(v[:, cols], first)
        outs = []
        for e in range(2):
            s = scored(queries[e], keys[e]) + bias
            p = jnp.exp(s - jnp.max(s, axis=1, keepdims=True))
            total = jnp.sum(p, axis=1, keepdims=True)
            outs.append(mixed_values(p, values[e]) / total)
        tiles.append(jnp.where(first, outs[0], outs[1]))
    return jnp.concatenate(tiles, axis=1)


def row_bias(first_row):
    row = iota((1, KEYS), 1) // SLOTS - 3 + first_row
    return jnp.where((row >= 0) & (row < HEIGHT), 0.0, NEG)


def places():
    return lax.axis_index(ROW_AXIS) * ROWS, lax.axis_index(COL_AXIS) * COLS


def middle_kernel(
    x_ref, left_ref, right_ref, q_ref, k_ref, v_ref, gain_ref, wp_ref, wo_ref,
    kw_ref, vw_ref, l0_ref, side,
):
    side[...] = jnp.zeros((ROWS, 8, C0), F32)
    side[:, 0:3, :] = right_ref[...]
    side[:, 3:6, :] = left_ref[...]
    k_side, v_side = keys_values(side[...].reshape(ROWS * 8, C0), gain_ref, wp_ref)
    for ref, own, extra in ((kw_ref, k_ref, k_side), (vw_ref, v_ref, v_side)):
        ref[0], ref[1] = windowed(own[...], extra.reshape(ROWS, 8, C0))
    first_row, first_col = places()
    masks = near_masks(first_col)
    first = iota((1, 128), 1) < HEAD
    for t in (1, 2):
        rows = slice(BLOCK * t, BLOCK * t + BLOCK)
        at = BLOCK * t - 3
        q = q_ref[BLOCK * t * COLS : BLOCK * (t + 1) * COLS, :].reshape(BLOCK, COLS, C0)
        outs = []
        for half in range(2):
            k = kw_ref[half, at : at + WINDOW].reshape(KEYS, C0)
            v = vw_ref[half, at : at + WINDOW].reshape(KEYS, C0)
            now = q[:, half * HALF : (half + 1) * HALF].reshape(QUERIES, C0)
            bias = masks[half] + row_bias(first_row + BLOCK * t)
            outs.append(window_block(now, k, v, bias, first).reshape(BLOCK, HALF, C0))
        attended = jnp.concatenate(outs, axis=1).reshape(BLOCK * COLS, C0)
        l0_ref[BLOCK * COLS * (t - 1) : BLOCK * COLS * t, :] = x_ref[rows].reshape(
            BLOCK * COLS, C0
        ) + mm(attended, wo_ref[...])


def outer_kernel(
    x_ref, top_ref, bot_ref, q_ref, kw_ref, vw_ref, mid_ref, gain_ref, wp_ref, wo_ref,
    m1_ref, m2_ref, ggain_ref,
    l0_ref, l1_ref, l2_ref, one_ref, nx_ref, order,
):
    raw = jnp.concatenate([top_ref[...], bot_ref[...]], axis=0).reshape(240, C0)
    k_new, v_new = keys_values(raw, gain_ref, wp_ref)
    k_new = k_new.reshape(6, 40, C0)
    v_new = v_new.reshape(6, 40, C0)
    k_new = windowed(k_new[:, 0:COLS], k_new[:, COLS:])
    v_new = windowed(v_new[:, 0:COLS], v_new[:, COLS:])
    first_row, first_col = places()
    masks = near_masks(first_col)
    first = iota((1, 128), 1) < HEAD
    for t in (0, 3):
        q = q_ref[BLOCK * t * COLS : BLOCK * (t + 1) * COLS, :].reshape(BLOCK, COLS, C0)
        outs = []
        for half in range(2):
            if t == 0:
                k = jnp.concatenate([k_new[half][0:3], kw_ref[half, 0:7]], axis=0)
                v = jnp.concatenate([v_new[half][0:3], vw_ref[half, 0:7]], axis=0)
            else:
                k = jnp.concatenate([kw_ref[half, 9:16], k_new[half][3:6]], axis=0)
                v = jnp.concatenate([vw_ref[half, 9:16], v_new[half][3:6]], axis=0)
            now = q[:, half * HALF : (half + 1) * HALF].reshape(QUERIES, C0)
            bias = masks[half] + row_bias(first_row + BLOCK * t)
            block = window_block(now, k.reshape(KEYS, C0), v.reshape(KEYS, C0), bias, first)
            outs.append(block.reshape(BLOCK, HALF, C0))
        attended = jnp.concatenate(outs, axis=1).reshape(BLOCK * COLS, C0)
        level = x_ref[BLOCK * t : BLOCK * (t + 1)].reshape(BLOCK * COLS, C0) + mm(
            attended, wo_ref[...]
        )
        for half in range(2):
            l0_ref[half, BLOCK * COLS * t : BLOCK * COLS * (t + 1), :] = level[
                :, half * 128 : (half + 1) * 128
            ]
    for half in range(2):
        l0_ref[half, 128:384, :] = mid_ref[:, half * 128 : (half + 1) * 128]
    for n, (a1, b1, a2, b2) in enumerate(CLASSES):
        for i in range(4):
            start = (BLOCK * i + 2 * a2 + a1) * COLS + 2 * b2 + b1
            for half in range(2):
                order[n * 32 + i * 8 : n * 32 + i * 8 + 8, half * 128 : half * 128 + 128] = l0_ref[
                    half, pl.ds(start, 8, stride=4), :
                ]
    one = mm(order[0:128, :], m1_ref[0:C0, :])
    for n in range(1, 4):
        one = one + mm(order[n * 128 : (n + 1) * 128, :], m1_ref[n * C0 : (n + 1) * C0, :])
    l1_ref[...] = one
    two = mm(one[0:32], m2_ref[0:CM, :])
    for n in range(1, 4):
        two = two + mm(one[n * 32 : (n + 1) * 32], m2_ref[n * CM : (n + 1) * CM, :])
    l2_ref[...] = two
    normed_two = rms(two, ggain_ref[...])
    one_ref[...] = normed_two
    for n in range(16):
        nx_ref[n] = normed_two


def chunks_in(gp_hbm, weight, sems, width):
    copies = []
    for m in range(4):
        cols = slice(384 * m, 384 * m + width)
        copies.append(pltpu.make_async_copy(gp_hbm.at[:, cols], weight.at[:, cols], sems.at[m]))
        copies[-1].start()
    return copies


def query_kernel(x_ref, gp_hbm, scale_hbm, q_ref, weight, scale, sems):
    scale_in = pltpu.make_async_copy(scale_hbm, scale, sems.at[4])
    scale_in.start()
    copies = chunks_in(gp_hbm, weight, sems, 256)
    first = iota((1, 128), 1) < HEAD
    x = x_ref[...]
    scale_in.wait()
    factor = lanes_of(scale, HEADS_G)
    for g in range(2):
        tiles = []
        for m in (2 * g, 2 * g + 1):
            copies[m].wait()
            at = 384 * m
            tiles.append(jnp.where(first, weight[:, at : at + 128], weight[:, at + 128 : at + 256]))
        q = floored(mm(x, jnp.concatenate(tiles, axis=1), HIGHEST))
        q_ref[:, g * 256 : (g + 1) * 256] = q * factor[:, g * 256 : (g + 1) * 256]


def picked(gp_ref, one, other, first):
    tiles = []
    for m in range(4):
        at = 384 * m
        a = gp_ref[:, at + 128 * one : at + 128 * one + 128]
        b = gp_ref[:, at + 128 * other : at + 128 * other + 128]
        tiles.append(jnp.where(first, a, b))
    return jnp.concatenate(tiles, axis=1)


def attention_kernel(x_ref, q_ref, gp_ref, mine_ref, other_ref, kk, vv):
    first = iota((1, 128), 1) < HEAD
    x = x_ref[...].reshape(512, CG)
    kk[...] = floored(mm(x, picked(gp_ref, 2, 0, first)))
    vv[...] = mm(x, picked(gp_ref, 1, 2, first))
    lane = iota((256, 128), 1)
    extra = jnp.zeros((256, 128), F32)
    q = q_ref[...].reshape(256, CG)
    for m in range(4):
        cols = slice(m * 128, (m + 1) * 128)
        queries = pair_queries(q[:, cols], first)
        keys = pair_keys(kk[:, cols], first)
        values = pair_values(vv[:, cols], first)
        outs = []
        for e in range(2):
            s = scored(queries[e], keys[1 - e])
            best = jnp.max(s, axis=1, keepdims=True)
            p = jnp.exp(s - best)
            outs.append(mixed_values(p, values[e]))
            extra = jnp.where(lane == 2 * m + e, best, extra)
            extra = jnp.where(lane == 8 + 2 * m + e, jnp.sum(p, axis=1, keepdims=True), extra)
        both = jnp.where(first, outs[0], outs[1]).reshape(4, 2, 32, 128)
        mine_ref[:, :, cols] = both[:, 0]
        other_ref[:, :, cols] = both[:, 1]
    both = extra.reshape(4, 2, 32, 128)
    mine_ref[:, :, CG:] = both[:, 0]
    other_ref[:, :, CG:] = both[:, 1]


def spreader():
    return jnp.where(iota((128, CG), 0) == iota((128, CG), 1) // HEAD, 1.0, 0.0)


def merge_kernel(a_ref, b_ref, *out_refs):
    a = a_ref[...].reshape(128, CG + 128)
    b = b_ref[...].reshape(128, CG + 128)
    lane = iota((128, 128), 1)
    best = jnp.maximum(a[:, CG:], b[:, CG:])
    total = jnp.zeros((128, CG), F32)
    sums = jnp.zeros((128, 128), F32)
    for part in (a, b):
        extra = part[:, CG:]
        w = jnp.where(lane < 8, jnp.exp(extra - best), 0.0)
        sums = sums + w * pltpu.roll(extra, 120, 1)
        total = total + mm(w, spreader(), HIGHEST) * part[:, 0:CG]
    extra = jnp.where(lane < 8, best, pltpu.roll(sums, 8, 1))
    for n, ref in enumerate(out_refs):
        ref[:, 0:CG] = total[n * 32 : (n + 1) * 32]
        ref[:, CG:] = extra[n * 32 : (n + 1) * 32]


def tail_kernel(
    p0_ref, p1_ref, p2_ref, p3_ref, l0_ref, l1_ref, l2_ref, go_ref, s2_ref, s1_ref, out_ref, spread
):
    arrived = (p0_ref, p1_ref, p2_ref, p3_ref)
    best = p0_ref[:, CG:]
    for ref in arrived[1:]:
        best = jnp.maximum(best, ref[:, CG:])
    pick = spreader()
    lane = iota((32, 128), 1)
    total = jnp.zeros((32, CG), F32)
    sums = jnp.zeros((32, 128), F32)
    for ref in arrived:
        extra = ref[:, CG:]
        w = jnp.where(lane < 8, jnp.exp(extra - best), 0.0)
        sums = sums + w * pltpu.roll(extra, 120, 1)
        total = total + mm(w, pick, HIGHEST) * ref[:, 0:CG]
    inverse = jnp.where(lane < 8, 1.0 / jnp.where(lane < 8, sums, 1.0), 0.0)
    mixed = l2_ref[...] + mm(total * mm(inverse, pick, HIGHEST), go_ref[...])
    second = mm(mixed, s2_ref[...])
    up = jnp.concatenate(
        [l1_ref[n * 32 : (n + 1) * 32, :] + second[:, n * CM : (n + 1) * CM] for n in range(4)],
        axis=0,
    )
    first = mm(up, s1_ref[...])
    for a1, b1, a2, b2 in CLASSES:
        c1 = a1 * 2 + b1
        c2 = a2 * 2 + b2
        for i in range(4):
            start = (BLOCK * i + 2 * a2 + a1) * COLS + 2 * b2 + b1
            for half in range(2):
                at = c1 * C0 + half * 128
                spread[half, pl.ds(start, 8, stride=4), :] = first[
                    c2 * 32 + i * 8 : c2 * 32 + i * 8 + 8, at : at + 128
                ]
    for half in range(2):
        out_ref[:, :, half * 128 : half * 128 + 128] = (spread[half] + l0_ref[half]).reshape(
            ROWS, COLS, 128
        )


def f32(*shape):
    return jax.ShapeDtypeStruct(shape, F32)


def shift(n, step):
    return [(i, i + step) for i in range(n) if 0 <= i + step < n]


V = pl.BlockSpec(memory_space=pltpu.VMEM)
H = pl.BlockSpec(memory_space=pltpu.HBM)
DMA = pltpu.SemaphoreType.DMA


def call(kernel, ins, outs, scratch=(), us=1, megabytes=16):
    many = isinstance(outs, tuple)
    run = pl.pallas_call(
        kernel,
        compiler_params=pltpu.CompilerParams(vmem_limit_bytes=megabytes << 20),
        cost_estimate=pl.CostEstimate(
            flops=int(us * 4e8), transcendentals=0, bytes_accessed=1 << 20
        ),
        out_shape=outs,
        in_specs=[H if i == "h" else V for i in ins],
        out_specs=tuple(V for _ in outs) if many else V,
        scratch_shapes=[pltpu.VMEM(s, F32) if isinstance(s, tuple) else s for s in scratch],
    )

    def placed(*args):
        return run(
            *(
                pltpu.with_memory_space_constraint(a, pltpu.HBM) if i == "h" else a
                for i, a in zip(ins, args)
            )
        )

    return placed


def shards(
    latent, local_gain, local_project, local_output, local_scale, merge_first, merge_second,
    global_gain, global_project, global_output, global_scale, split_second, split_first,
):
    gain = local_gain[None]
    first, last = call(edge_kernel, "v", (f32(ROWS, 3, C0), f32(ROWS, 3, C0)))(latent)
    right = lax.ppermute(first, COL_AXIS, shift(16, -1))
    left = lax.ppermute(last, COL_AXIS, shift(16, 1))
    q, k, v = call(
        own_kernel,
        "vhhh",
        (f32(512, C0), f32(ROWS, COLS, C0), f32(ROWS, COLS, C0)),
        [(1, C0), (C0, 3 * C0), pltpu.SMEM((HEADS0,), F32), DMA((3,))],
        us=5,
    )(latent, gain, local_project, local_scale)
    up, down = call(row_kernel, "vvv", (f32(3, 40, C0), f32(3, 40, C0)))(latent, left, right)
    bot = lax.ppermute(up, ROW_AXIS, shift(8, -1))
    top = lax.ppermute(down, ROW_AXIS, shift(8, 1))
    kw, vw, mid = call(
        middle_kernel,
        "v" * 9,
        (f32(2, ROWS, SLOTS, C0), f32(2, ROWS, SLOTS, C0), f32(256, C0)),
        [(ROWS, 8, C0)],
        us=8,
    )(latent, left, right, q, k, v, gain, local_project, local_output)
    l0, l1, l2, one, nx = call(
        outer_kernel,
        "v" * 13,
        (f32(2, 512, 128), f32(128, CM), f32(32, CG), f32(32, CG), f32(16, 32, CG)),
        [(512, C0)],
    )(
        latent, top, bot, q, kw, vw, mid, gain, local_project, local_output,
        merge_first, merge_second, global_gain[None],
    )
    keys_from = lax.all_to_all(nx, ZX, 0, 0, tiled=True)
    qg = call(
        query_kernel,
        "vhh",
        f32(32, CG),
        [(CG, 3 * CG), pltpu.SMEM((HEADS_G,), F32), DMA((5,))],
        us=4,
    )(one, global_project, global_scale)
    swapped = lax.ppermute(qg, "c", [(0, 1), (1, 0)])
    two = jnp.stack([qg, swapped])
    around = [lax.ppermute(two, "y", [(i, (i + d) % 4) for i in range(4)]) for d in TURNS]
    queries_from = jnp.concatenate([two] + around)
    mine, other = call(
        attention_kernel,
        "vvv",
        (f32(4, 32, CG + 128), f32(4, 32, CG + 128)),
        [(512, CG), (512, CG)],
    )(keys_from, queries_from, global_project)
    theirs = lax.ppermute(other, "c", [(0, 1), (1, 0)])
    merged = call(merge_kernel, "vv", tuple(f32(32, CG + 128) for _ in range(4)))(mine, theirs)
    arrived = [merged[0]] + [
        lax.ppermute(part, "y", [(i, (i - d) % 4) for i in range(4)])
        for part, d in zip(merged[1:], TURNS)
    ]
    return call(tail_kernel, "v" * 10, f32(ROWS, COLS, C0), [(2, 512, 128)])(
        *arrived, l0, l1, l2, global_output, split_second, split_first
    )


def solution(mesh):
    fine = Mesh(mesh.devices.reshape(4, 2, 4, 2, 2), ("z", "xl", "y", "xh", "c"))
    tile = P(ROW_AXIS, COL_AXIS, None)
    return jax.shard_map(
        shards, mesh=fine, in_specs=(tile,) + (P(),) * 12, out_specs=tile, check_vma=False
    )
```

time: 135 us -> 80.2 us (0.59)
  blocking collectives: 33.6 us -> 0 us
  local copies, waits for them, and re-layouts: 16.5 us -> 3.02 us
  Pallas kernels: 33.8 us -> 29.2 us
  starting transfers between devices: 36.1 us -> 33.4 us
    all_to_all x2 -> x0, blocking collectives: 33.6 us -> none  [the longest x1 18 us: shards(): part = lax.all_to_all(part, YC, 0, 0, tiled=True)]
    ppermute x8 -> x12, waiting for transfers between devices: 0.52 us -> 11.6 us  [the longest x3 4.96 us: shards(): lax.ppermute(two, 'y', [(i, (i + d) % 4) for i in range(4)])]
    all_to_all x1, waiting for transfers between devices: 13 us -> 2 us  [shards(): keys_from = lax.all_to_all(nx, ZX, 0, 0, tiled=True)]
    another operation x5 -> x0, local copies, waits for them, and re-layouts: 6.49 us -> none  [the longest x1 2.52 us: shards(): wq = split[:, :, 0].reshape(CG, CG)]
    slice x4 -> x0, local copies, waits for them, and re-layouts: 5.76 us -> none  [the longest x1 1.77 us: shards(): wv = split[:, :, 2].reshape(CG, CG)]
    pallas_call x3 -> x9, Pallas kernels: 33.8 us -> 29.2 us  [placed(): run(*(pltpu.with_memory_space_constraint(a, pltpu.HBM) if i == 'h' else a...]
    all_to_all x1, starting transfers between devices: 11.8 us -> 9.66 us  [shards(): keys_from = lax.all_to_all(nx, ZX, 0, 0, tiled=True)]
    unnamed x27 -> x26, local copies, waits for them, and re-layouts: 4.07 us -> 3.01 us
  transfers between devices with their start and end apart: 9 -> 13, of which waited for: 2 -> 8; matrix products, arithmetic and copies ran while one was open for 10% -> 0% of each run, Pallas kernels for 0% -> 15%
where the time goes in v1:
time: 80.2 us; the launch traced here: 79.4 us
  starting transfers between devices  33.4 us (42%)
  Pallas kernels  29.2 us (36%)
  waiting for transfers between devices  13.6 us (17%)
  local copies, waits for them, and re-layouts  3.02 us (4%)
    pallas_call x9, Pallas kernels, placed(): run(*(pltpu.with_memory_space_constraint(a, pltpu.HBM) if i == 'h' else a...  29.2 us
    all_to_all x1, starting transfers between devices, shards(): keys_from = lax.all_to_all(nx, ZX, 0, 0, tiled=True)  9.66 us
    ppermute x1, starting transfers between devices, shards(): left = lax.ppermute(last, COL_AXIS, shift(16, 1))  6.03 us
    ppermute x3, waiting for transfers between devices, shards(): lax.ppermute(two, 'y', [(i, (i + d) % 4) for i in range(4)])  4.96 us
    ppermute x3, starting transfers between devices, shards(): lax.ppermute(two, 'y', [(i, (i + d) % 4) for i in range(4)])  4.45 us
    ppermute x3, starting transfers between devices, shards(): lax.ppermute(part, 'y', [(i, (i - d) % 4) for i in range(4)])  4.16 us
    ppermute x3, waiting for transfers between devices, shards(): lax.ppermute(part, 'y', [(i, (i - d) % 4) for i in range(4)])  3.34 us
    unnamed x26, local copies, waits for them, and re-layouts  3.01 us
  transfers between devices with their start and end apart: 13, of which 8 were waited for; matrix products, arithmetic and copies ran while one was open for 0% of the time, Pallas kernels for 15%

profile of v1, /device:TPU:1, one launch (start us, length us, event | category | flops | bytes accessed | tf_op | source)
XLA Modules:
  0.0 79.4 jit_solution(1023315666124368454)
XLA Ops:
  0.0 1.0 %copy-done.7 = f32[16,32,256]{2,1,0:T(8,128)S(1)} copy-done((f32[16,32,256]{2,1,0:T(8,128)S(1)}, f32[16,32,256]{2,1,0:T(8,128)}, u32[]{:S(2)}) %copy-start.7) | copy-done | bytes 524312
  1.1 6.0 %collective-permute-start = (f32[16,3,256]{2,1,0:T(4,128)S(1)}, f32[16,3,256]{2,1,0:T(4,128)S(1)}, u32[]{:S(2)}, u32[]{:S(2)}) collective-permute-start(f32[16,3,256]{2,1,0:T(4,128)S(1)} %get-tuple-element.26), channel_id=1, source_target_pairs={{0,1},{1,2},{2,3},{3,4},{4,5},{5,6},{6,7},{7,8},{8,9},{9,10},{10,1... | collective-permute-start | bytes 147464 | tf_op jit(solution)/shard_map/ppermute | solution.py:478
  7.1 1.9 %collective-permute-start.1 = (f32[16,3,256]{2,1,0:T(4,128)S(1)}, f32[16,3,256]{2,1,0:T(4,128)S(1)}, u32[]{:S(2)}, u32[]{:S(2)}) collective-permute-start(f32[16,3,256]{2,1,0:T(4,128)S(1)} %get-tuple-element.27), channel_id=1, source_target_pairs={{1,0},{2,1},{3,2},{4,3},{5,4},{6,5},{7,6},{8,7},{9,8},{10,9},{11,1... | collective-permute-start | bytes 147464 | tf_op jit(solution)/shard_map/ppermute | solution.py:477
  9.0 0.0 copy-start.6
  9.1 3.9 %shard_map.129 = (f32[512,256]{1,0:T(8,128)S(1)}, f32[16,32,256]{2,1,0:T(8,128)S(1)}, f32[16,32,256]{2,1,0:T(8,128)S(1)}) custom-call(f32[16,32,256]{2,1,0:T(8,128)S(1)} %copy-done.7, f32[1,256]{1,0:T(1,128)} %bitcast.8, f32[256,768]{1,0:T(8,128)} %wp_ref.3, f32[4]{0:T(128)} %scale_hbm.2), custom_call_target="tpu_custom_call" | custom-call | flops 2000000000 | bytes 1048576 | tf_op jit(solution)/shard_map/pallas_call | solution.py:461
  13.0 1.2 %collective-permute-done.1.right_ref = f32[16,3,256]{2,1,0:T(4,128)S(1)} collective-permute-done((f32[16,3,256]{2,1,0:T(4,128)S(1)}, f32[16,3,256]{2,1,0:T(4,128)S(1)}, u32[]{:S(2)}, u32[]{:S(2)}) %collective-permute-start.1) | collective-permute-done | bytes 49184 | tf_op jit(solution)/shard_map/ppermute | solution.py:477
  14.2 2.2 %collective-permute-start.2 = (f32[3,40,256]{2,1,0:T(8,128)S(1)}, f32[3,40,256]{2,1,0:T(8,128)S(1)}, u32[]{:S(2)}, u32[]{:S(2)}) collective-permute-start(f32[3,40,256]{2,1,0:T(8,128)S(1)} %get-tuple-element.28), channel_id=1, source_target_pairs={{0,16},{16,32},{32,48},{48,64},{64,80},{80,96},{96,112},{1,17},{17... | collective-permute-start | bytes 368648 | tf_op jit(solution)/shard_map/ppermute | solution.py:488
  16.5 1.3 %collective-permute-start.3 = (f32[3,40,256]{2,1,0:T(8,128)S(1)}, f32[3,40,256]{2,1,0:T(8,128)S(1)}, u32[]{:S(2)}, u32[]{:S(2)}) collective-permute-start(f32[3,40,256]{2,1,0:T(8,128)S(1)} %get-tuple-element.29), channel_id=1, source_target_pairs={{16,0},{32,16},{48,32},{64,48},{80,64},{96,80},{112,96},{17,1},{33... | collective-permute-start | bytes 368648 | tf_op jit(solution)/shard_map/ppermute | solution.py:487
  17.8 0.0 copy-start.4
  17.8 5.4 %shard_map.130 = (f32[2,16,24,256]{3,2,1,0:T(8,128)S(1)}, f32[2,16,24,256]{3,2,1,0:T(8,128)S(1)}, f32[256,256]{1,0:T(8,128)S(1)}) custom-call(f32[16,32,256]{2,1,0:T(8,128)S(1)} %copy-done.7, f32[16,3,256]{2,1,0:T(4,128)S(1)} %collective-permute-done.left_ref, f32[16,3,256]{2,1,0:T(4,128)S(1)} %collective-permute-done.1.right_ref, ...), custom_call_target="tpu_custom_call" | custom-call | flops 3200000000 | bytes 1048576 | tf_op jit(solution)/shard_map/pallas_call | solution.py:461
  23.3 7.9 %shard_map.131 = (f32[2,512,128]{2,1,0:T(8,128)S(1)}, f32[128,384]{1,0:T(8,128)S(1)}, f32[32,512]{1,0:T(8,128)S(1)}, f32[32,512]{1,0:T(8,128)S(1)}, f32[16,32,512]{2,1,0:T(8,128)}) custom-call(f32[16,32,256]{2,1,0:T(8,128)S(1)} %copy-done.7, f32[3,40,256]{2,1,0:T(8,128)S(1)} %collective-permute-done.2.top_ref, ...), custom_call_target="tpu_custom_call" | custom-call | flops 400000000 | bytes 1048576 | tf_op jit(solution)/shard_map/pallas_call | solution.py:461
  31.2 9.7 %all-to-all-start = ((f32[16,32,512]{2,1,0:T(8,128)}), f32[16,32,512]{2,1,0:T(8,128)S(1)}, u32[]{:S(2)}, u32[]{:S(2)}) async-start(f32[16,32,512]{2,1,0:T(8,128)} %get-tuple-element.36), calls=%async_computation | async-start | bytes 2097152 | tf_op jit(solution)/shard_map/all_to_all | solution.py:505
  40.9 2.7 %shard_map.132 = f32[32,512]{1,0:T(8,128)S(1)} custom-call(f32[32,512]{1,0:T(8,128)S(1)} %get-tuple-element.37.x_ref, f32[512,1536]{1,0:T(8,128)} %gp_ref.1, f32[8]{0:T(128)} %scale_hbm.3), custom_call_target="tpu_custom_call" | custom-call | flops 1600000000 | bytes 1048576 | tf_op jit(solution)/shard_map/pallas_call | solution.py:461
  43.6 1.0 %collective-permute-start.4 = (f32[32,512]{1,0:T(8,128)S(1)}, f32[32,512]{1,0:T(8,128)S(1)}, u32[]{:S(2)}, u32[]{:S(2)}) collective-permute-start(f32[32,512]{1,0:T(8,128)S(1)} %shard_map.132), channel_id=1, source_target_pairs={{0,1},{1,0},{2,3},{3,2},{4,5},{5,4},{6,7},{7,6},{8,9},{9,8},{10,11... | collective-permute-start | bytes 196616 | tf_op jit(solution)/shard_map/ppermute | solution.py:513
  44.6 0.9 %collective-permute-done.4 = f32[32,512]{1,0:T(8,128)S(1)} collective-permute-done((f32[32,512]{1,0:T(8,128)S(1)}, f32[32,512]{1,0:T(8,128)S(1)}, u32[]{:S(2)}, u32[]{:S(2)}) %collective-permute-start.4) | collective-permute-done | bytes 65568 | tf_op jit(solution)/shard_map/ppermute | solution.py:513
  45.5 3.0 %collective-permute-start.7 = (f32[2,32,512]{2,1,0:T(8,128)S(1)}, f32[2,32,512]{2,1,0:T(8,128)S(1)}, u32[]{:S(2)}, u32[]{:S(2)}) collective-permute-start(f32[2,32,512]{2,1,0:T(8,128)S(1)} %pad_maximum_fusion), channel_id=1, source_target_pairs={{0,8},{4,12},{8,0},{12,4},{1,9},{5,13},{9,1},{13,5},{2,10},{6,14},... | collective-permute-start | bytes 393224 | tf_op jit(solution)/shard_map/ppermute | solution.py:515
  48.5 0.8 collective-permute-start.6
  49.2 0.7 collective-permute-start.5
  49.9 4.8 %collective-permute-done.5 = f32[2,32,512]{2,1,0:T(8,128)S(1)} collective-permute-done((f32[2,32,512]{2,1,0:T(8,128)S(1)}, f32[2,32,512]{2,1,0:T(8,128)S(1)}, u32[]{:S(2)}, u32[]{:S(2)}) %collective-permute-start.5) | collective-permute-done | bytes 131104 | tf_op jit(solution)/shard_map/ppermute | solution.py:515
  54.7 0.2 collective-permute-done.6
  54.9 2.0 %all-to-all-done.x_ref = f32[16,32,512]{2,1,0:T(8,128)S(1)} async-done(((f32[16,32,512]{2,1,0:T(8,128)}), f32[16,32,512]{2,1,0:T(8,128)S(1)}, u32[]{:S(2)}, u32[]{:S(2)}) %all-to-all-start) | async-done | bytes 1048608 | tf_op jit(solution)/shard_map/all_to_all | solution.py:505
  56.9 1.9 %copy-done.1 = f32[512,1536]{1,0:T(8,128)S(1)} copy-done((f32[512,1536]{1,0:T(8,128)S(1)}, f32[512,1536]{1,0:T(8,128)}, u32[]{:S(2)}) %copy-start.1) | copy-done | bytes 3145752
  58.8 5.3 %shard_map.133 = (f32[4,32,640]{2,1,0:T(8,128)S(1)}, f32[4,32,640]{2,1,0:T(8,128)S(1)}) custom-call(f32[16,32,512]{2,1,0:T(8,128)S(1)} %all-to-all-done.x_ref, f32[8,32,512]{2,1,0:T(8,128)S(1)} %constant_dynamic-update-slice_fusion.q_ref, f32[512,1536]{1,0:T(8,128)S(1)} %copy-done.1), custom_call_target="tpu_custom_call" | custom-call | flops 400000000 | bytes 1048576 | tf_op jit(solution)/shard_map/pallas_call | solution.py:461
  64.1 2.6 %collective-permute-start.8 = (f32[4,32,640]{2,1,0:T(8,128)S(1)}, f32[4,32,640]{2,1,0:T(8,128)S(1)}, u32[]{:S(2)}, u32[]{:S(2)}) collective-permute-start(f32[4,32,640]{2,1,0:T(8,128)S(1)} %get-tuple-element.39), channel_id=1, source_target_pairs={{0,1},{1,0},{2,3},{3,2},{4,5},{5,4},{6,7},{7,6},{8,9},{9,8},{10,11... | collective-permute-start | bytes 983048 | tf_op jit(solution)/shard_map/ppermute | solution.py:523
  66.8 1.3 %collective-permute-done.8.b_ref = f32[4,32,640]{2,1,0:T(8,128)S(1)} collective-permute-done((f32[4,32,640]{2,1,0:T(8,128)S(1)}, f32[4,32,640]{2,1,0:T(8,128)S(1)}, u32[]{:S(2)}, u32[]{:S(2)}) %collective-permute-start.8) | collective-permute-done | bytes 327712 | tf_op jit(solution)/shard_map/ppermute | solution.py:523
  68.0 0.6 shard_map.134
  68.6 0.8 %collective-permute-start.9 = (f32[32,640]{1,0:T(8,128)S(1)}, f32[32,640]{1,0:T(8,128)S(1)}, u32[]{:S(2)}, u32[]{:S(2)}) collective-permute-start(f32[32,640]{1,0:T(8,128)S(1)} %get-tuple-element.41), channel_id=1, source_target_pairs={{0,12},{4,0},{8,4},{12,8},{1,13},{5,1},{9,5},{13,9},{2,14},{6,2},{... | collective-permute-start | bytes 245768 | tf_op jit(solution)/shard_map/ppermute | solution.py:526
  69.4 0.7 collective-permute-start.10
  70.1 2.6 %collective-permute-start.11 = (f32[32,640]{1,0:T(8,128)S(1)}, f32[32,640]{1,0:T(8,128)S(1)}, u32[]{:S(2)}, u32[]{:S(2)}) collective-permute-start(f32[32,640]{1,0:T(8,128)S(1)} %get-tuple-element.43), channel_id=1, source_target_pairs={{0,8},{4,12},{8,0},{12,4},{1,9},{5,13},{9,1},{13,5},{2,10},{6,14},... | collective-permute-start | bytes 245768 | tf_op jit(solution)/shard_map/ppermute | solution.py:526
  72.8 1.2 %collective-permute-done.10.p2_ref = f32[32,640]{1,0:T(8,128)S(1)} collective-permute-done((f32[32,640]{1,0:T(8,128)S(1)}, f32[32,640]{1,0:T(8,128)S(1)}, u32[]{:S(2)}, u32[]{:S(2)}) %collective-permute-start.10) | collective-permute-done | bytes 81952 | tf_op jit(solution)/shard_map/ppermute | solution.py:526
  73.9 2.2 %collective-permute-done.11.p3_ref = f32[32,640]{1,0:T(8,128)S(1)} collective-permute-done((f32[32,640]{1,0:T(8,128)S(1)}, f32[32,640]{1,0:T(8,128)S(1)}, u32[]{:S(2)}, u32[]{:S(2)}) %collective-permute-start.11) | collective-permute-done | bytes 81952 | tf_op jit(solution)/shard_map/ppermute | solution.py:526
  76.1 3.3 %shard_map.135 = f32[16,32,256]{2,1,0:T(8,128)} custom-call(f32[32,640]{1,0:T(8,128)S(1)} %get-tuple-element.40.p0_ref, f32[32,640]{1,0:T(8,128)S(1)} %collective-permute-done.9.p1_ref, f32[32,640]{1,0:T(8,128)S(1)} %collective-permute-done.10.p2_ref, f32[32,640]{1,0:T(8,128)S(1)} %collective-permute-done.11.p3_ref, ...), custom_call_target="tpu_custom_call" | custom-call | flops 400000000 | bytes 1048576 | tf_op jit(solution)/shard_map/pallas_call | solution.py:461
  (31 shorter events, 0.2 us)
Async XLA Ops:
  0.0 1.0 %copy-start.7 = (f32[16,32,256]{2,1,0:T(8,128)S(1)}, f32[16,32,256]{2,1,0:T(8,128)}, u32[]{:S(2)}) copy-start(f32[16,32,256]{2,1,0:T(8,128)} %x_ref.9) | copy-start | bytes 1572868
  1.1 12.0 %collective-permute-start = (f32[16,3,256]{2,1,0:T(4,128)S(1)}, f32[16,3,256]{2,1,0:T(4,128)S(1)}, u32[]{:S(2)}, u32[]{:S(2)}) collective-permute-start(f32[16,3,256]{2,1,0:T(4,128)S(1)} %get-tuple-element.26), channel_id=1, source_target_pairs={{0,1},{1,2},{2,3},{3,4},{4,5},{5,6},{6,7},{7,8},{8,9},{9,10},{10,1... | collective-permute-start | bytes 147464 | tf_op jit(solution)/shard_map/ppermute | solution.py:478
  7.1 7.1 %collective-permute-start.1 = (f32[16,3,256]{2,1,0:T(4,128)S(1)}, f32[16,3,256]{2,1,0:T(4,128)S(1)}, u32[]{:S(2)}, u32[]{:S(2)}) collective-permute-start(f32[16,3,256]{2,1,0:T(4,128)S(1)} %get-tuple-element.27), channel_id=1, source_target_pairs={{1,0},{2,1},{3,2},{4,3},{5,4},{6,5},{7,6},{8,7},{9,8},{10,9},{11,1... | collective-permute-start | bytes 147464 | tf_op jit(solution)/shard_map/ppermute | solution.py:477
  9.0 8.7 %copy-start.6 = (f32[256,768]{1,0:T(8,128)S(1)}, f32[256,768]{1,0:T(8,128)}, u32[]{:S(2)}) copy-start(f32[256,768]{1,0:T(8,128)} %wp_ref.3) | copy-start | bytes 2359300
  9.0 8.7 %copy-start.8 = (f32[256,256]{1,0:T(8,128)S(1)}, f32[256,256]{1,0:T(8,128)}, u32[]{:S(2)}) copy-start(f32[256,256]{1,0:T(8,128)} %wo_ref.3) | copy-start | bytes 786436
  9.1 8.7 %copy-start.10 = (f32[256]{0:T(256)S(1)}, f32[256]{0:T(256)}, u32[]{:S(2)}) copy-start(f32[256]{0:T(256)} %param.14) | copy-start | bytes 3076
  14.2 9.0 %collective-permute-start.2 = (f32[3,40,256]{2,1,0:T(8,128)S(1)}, f32[3,40,256]{2,1,0:T(8,128)S(1)}, u32[]{:S(2)}, u32[]{:S(2)}) collective-permute-start(f32[3,40,256]{2,1,0:T(8,128)S(1)} %get-tuple-element.28), channel_id=1, source_target_pairs={{0,16},{16,32},{32,48},{48,64},{64,80},{80,96},{96,112},{1,17},{17... | collective-permute-start | bytes 368648 | tf_op jit(solution)/shard_map/ppermute | solution.py:488
  16.5 6.8 %collective-permute-start.3 = (f32[3,40,256]{2,1,0:T(8,128)S(1)}, f32[3,40,256]{2,1,0:T(8,128)S(1)}, u32[]{:S(2)}, u32[]{:S(2)}) collective-permute-start(f32[3,40,256]{2,1,0:T(8,128)S(1)} %get-tuple-element.29), channel_id=1, source_target_pairs={{16,0},{32,16},{48,32},{64,48},{80,64},{96,80},{112,96},{17,1},{33... | collective-permute-start | bytes 368648 | tf_op jit(solution)/shard_map/ppermute | solution.py:487
  17.8 5.5 %copy-start.2 = (f32[1536,512]{1,0:T(8,128)S(1)}, f32[1536,512]{1,0:T(8,128)}, u32[]{:S(2)}) copy-start(f32[1536,512]{1,0:T(8,128)} %m2_ref.1) | copy-start | bytes 9437188
  17.8 5.5 %copy-start.4 = (f32[1024,384]{1,0:T(8,128)S(1)}, f32[1024,384]{1,0:T(8,128)}, u32[]{:S(2)}) copy-start(f32[1024,384]{1,0:T(8,128)} %m1_ref.1) | copy-start | bytes 4718596
  17.8 5.5 %copy-start.9 = (f32[512]{0:T(512)S(1)}, f32[512]{0:T(512)}, u32[]{:S(2)}) copy-start(f32[512]{0:T(512)} %param.20) | copy-start | bytes 6148
  31.2 25.7 %all-to-all-start = ((f32[16,32,512]{2,1,0:T(8,128)}), f32[16,32,512]{2,1,0:T(8,128)S(1)}, u32[]{:S(2)}, u32[]{:S(2)}) async-start(f32[16,32,512]{2,1,0:T(8,128)} %get-tuple-element.36), calls=%async_computation | async-start | bytes 2097152 | tf_op jit(solution)/shard_map/all_to_all | solution.py:505
  43.6 1.9 %collective-permute-start.4 = (f32[32,512]{1,0:T(8,128)S(1)}, f32[32,512]{1,0:T(8,128)S(1)}, u32[]{:S(2)}, u32[]{:S(2)}) collective-permute-start(f32[32,512]{1,0:T(8,128)S(1)} %shard_map.132), channel_id=1, source_target_pairs={{0,1},{1,0},{2,3},{3,2},{4,5},{5,4},{6,7},{7,6},{8,9},{9,8},{10,11... | collective-permute-start | bytes 196616 | tf_op jit(solution)/shard_map/ppermute | solution.py:513
  45.5 9.4 %collective-permute-start.7 = (f32[2,32,512]{2,1,0:T(8,128)S(1)}, f32[2,32,512]{2,1,0:T(8,128)S(1)}, u32[]{:S(2)}, u32[]{:S(2)}) collective-permute-start(f32[2,32,512]{2,1,0:T(8,128)S(1)} %pad_maximum_fusion), channel_id=1, source_target_pairs={{0,8},{4,12},{8,0},{12,4},{1,9},{5,13},{9,1},{13,5},{2,10},{6,14},... | collective-permute-start | bytes 393224 | tf_op jit(solution)/shard_map/ppermute | solution.py:515
  48.5 6.4 %collective-permute-start.6 = (f32[2,32,512]{2,1,0:T(8,128)S(1)}, f32[2,32,512]{2,1,0:T(8,128)S(1)}, u32[]{:S(2)}, u32[]{:S(2)}) collective-permute-start(f32[2,32,512]{2,1,0:T(8,128)S(1)} %pad_maximum_fusion), channel_id=1, source_target_pairs={{0,12},{4,0},{8,4},{12,8},{1,13},{5,1},{9,5},{13,9},{2,14},{6,2},{... | collective-permute-start | bytes 393224 | tf_op jit(solution)/shard_map/ppermute | solution.py:515
  49.2 5.5 %collective-permute-start.5 = (f32[2,32,512]{2,1,0:T(8,128)S(1)}, f32[2,32,512]{2,1,0:T(8,128)S(1)}, u32[]{:S(2)}, u32[]{:S(2)}) collective-permute-start(f32[2,32,512]{2,1,0:T(8,128)S(1)} %pad_maximum_fusion), channel_id=1, source_target_pairs={{0,4},{4,8},{8,12},{12,0},{1,5},{5,9},{9,13},{13,1},{2,6},{6,10},{... | collective-permute-start | bytes 393224 | tf_op jit(solution)/shard_map/ppermute | solution.py:515
  56.9 1.9 %copy-start.1 = (f32[512,1536]{1,0:T(8,128)S(1)}, f32[512,1536]{1,0:T(8,128)}, u32[]{:S(2)}) copy-start(f32[512,1536]{1,0:T(8,128)} %gp_ref.1) | copy-start | bytes 9437188
  58.8 17.3 %copy-start = (f32[512,1536]{1,0:T(8,128)S(1)}, f32[512,1536]{1,0:T(8,128)}, u32[]{:S(2)}) copy-start(f32[512,1536]{1,0:T(8,128)} %s2_ref.1) | copy-start | bytes 9437188
  58.8 17.3 %copy-start.3 = (f32[384,1024]{1,0:T(8,128)S(1)}, f32[384,1024]{1,0:T(8,128)}, u32[]{:S(2)}) copy-start(f32[384,1024]{1,0:T(8,128)} %s1_ref.1) | copy-start | bytes 4718596
  58.8 17.3 %copy-start.5 = (f32[512,512]{1,0:T(8,128)S(1)}, f32[512,512]{1,0:T(8,128)}, u32[]{:S(2)}) copy-start(f32[512,512]{1,0:T(8,128)} %go_ref.1) | copy-start | bytes 3145732
  64.1 3.9 %collective-permute-start.8 = (f32[4,32,640]{2,1,0:T(8,128)S(1)}, f32[4,32,640]{2,1,0:T(8,128)S(1)}, u32[]{:S(2)}, u32[]{:S(2)}) collective-permute-start(f32[4,32,640]{2,1,0:T(8,128)S(1)} %get-tuple-element.39), channel_id=1, source_target_pairs={{0,1},{1,0},{2,3},{3,2},{4,5},{5,4},{6,7},{7,6},{8,9},{9,8},{10,11... | collective-permute-start | bytes 983048 | tf_op jit(solution)/shard_map/ppermute | solution.py:523
  68.6 4.2 %collective-permute-start.9 = (f32[32,640]{1,0:T(8,128)S(1)}, f32[32,640]{1,0:T(8,128)S(1)}, u32[]{:S(2)}, u32[]{:S(2)}) collective-permute-start(f32[32,640]{1,0:T(8,128)S(1)} %get-tuple-element.41), channel_id=1, source_target_pairs={{0,12},{4,0},{8,4},{12,8},{1,13},{5,1},{9,5},{13,9},{2,14},{6,2},{... | collective-permute-start | bytes 245768 | tf_op jit(solution)/shard_map/ppermute | solution.py:526
  69.4 4.5 %collective-permute-start.10 = (f32[32,640]{1,0:T(8,128)S(1)}, f32[32,640]{1,0:T(8,128)S(1)}, u32[]{:S(2)}, u32[]{:S(2)}) collective-permute-start(f32[32,640]{1,0:T(8,128)S(1)} %get-tuple-element.42), channel_id=1, source_target_pairs={{0,4},{4,8},{8,12},{12,0},{1,5},{5,9},{9,13},{13,1},{2,6},{6,10},{... | collective-permute-start | bytes 245768 | tf_op jit(solution)/shard_map/ppermute | solution.py:526
  70.1 6.0 %collective-permute-start.11 = (f32[32,640]{1,0:T(8,128)S(1)}, f32[32,640]{1,0:T(8,128)S(1)}, u32[]{:S(2)}, u32[]{:S(2)}) collective-permute-start(f32[32,640]{1,0:T(8,128)S(1)} %get-tuple-element.43), channel_id=1, source_target_pairs={{0,8},{4,12},{8,0},{12,4},{1,9},{5,13},{9,1},{13,5},{2,10},{6,14},... | collective-permute-start | bytes 245768 | tf_op jit(solution)/shard_map/ppermute | solution.py:526

commit v2 on v1

--- a/solution.py
+++ b/solution.py
@@ -117,17 +117,31 @@
     return r + pltpu.roll(r, HEAD, 1)
 
 
-def edge_kernel(x_ref, first_ref, last_ref):
-    first_ref[...] = x_ref[:, 0:3, :]
-    last_ref[...] = x_ref[:, COLS - 3 : COLS, :]
-
-
-def row_kernel(x_ref, left_ref, right_ref, up_ref, down_ref):
-    for ref, at in ((up_ref, 0), (down_ref, ROWS - 3)):
-        ref[:, 0:COLS, :] = x_ref[at : at + 3]
+def edge_kernel(x_ref, inner_ref, outer_ref):
+    even = lax.axis_index("c") == 0
+    first = x_ref[:, 0:3, :]
+    last = x_ref[:, COLS - 3 : COLS, :]
+    inner_ref[...] = jnp.where(even, last, first)
+    outer_ref[...] = jnp.where(even, first, last)
+
+
+def sides(inner_ref, outer_ref):
+    even = lax.axis_index("c") == 0
+    inner = inner_ref[...]
+    outer = outer_ref[...]
+    return jnp.where(even, outer, inner), jnp.where(even, inner, outer)
+
+
+def row_kernel(x_ref, in_ref, out_ref, inner_ref, outer_ref):
+    left, right = sides(in_ref, out_ref)
+    even = lax.axis_index("xl") == 0
+    x_first = x_ref[0:3]
+    x_last = x_ref[ROWS - 3 : ROWS]
+    for ref, down in ((inner_ref, even), (outer_ref, jnp.logical_not(even))):
+        ref[:, 0:COLS, :] = jnp.where(down, x_last, x_first)
         ref[:, COLS : COLS + 8, :] = jnp.zeros((3, 8, C0), F32)
-        ref[:, COLS : COLS + 3, :] = right_ref[at : at + 3]
-        ref[:, COLS + 3 : COLS + 6, :] = left_ref[at : at + 3]
+        ref[:, COLS : COLS + 3, :] = jnp.where(down, right[ROWS - 3 :], right[0:3])
+        ref[:, COLS + 3 : COLS + 6, :] = jnp.where(down, left[ROWS - 3 :], left[0:3])
 
 
 def own_kernel(
@@ -214,12 +228,13 @@
 
 
 def middle_kernel(
-    x_ref, left_ref, right_ref, q_ref, k_ref, v_ref, gain_ref, wp_ref, wo_ref,
+    x_ref, in_ref, out_ref, q_ref, k_ref, v_ref, gain_ref, wp_ref, wo_ref,
     kw_ref, vw_ref, l0_ref, side,
 ):
     side[...] = jnp.zeros((ROWS, 8, C0), F32)
-    side[:, 0:3, :] = right_ref[...]
-    side[:, 3:6, :] = left_ref[...]
+    left, right = sides(in_ref, out_ref)
+    side[:, 0:3, :] = right
+    side[:, 3:6, :] = left
     k_side, v_side = keys_values(side[...].reshape(ROWS * 8, C0), gain_ref, wp_ref)
     for ref, own, extra in ((kw_ref, k_ref, k_side), (vw_ref, v_ref, v_side)):
         ref[0], ref[1] = windowed(own[...], extra.reshape(ROWS, 8, C0))
@@ -244,11 +259,14 @@
 
 
 def outer_kernel(
-    x_ref, top_ref, bot_ref, q_ref, kw_ref, vw_ref, mid_ref, gain_ref, wp_ref, wo_ref,
+    x_ref, in_ref, out_ref, q_ref, kw_ref, vw_ref, mid_ref, gain_ref, wp_ref, wo_ref,
     m1_ref, m2_ref, ggain_ref,
     l0_ref, l1_ref, l2_ref, one_ref, nx_ref, order,
 ):
-    raw = jnp.concatenate([top_ref[...], bot_ref[...]], axis=0).reshape(240, C0)
+    even = lax.axis_index("xl") == 0
+    top = jnp.where(even, out_ref[...], in_ref[...])
+    bot = jnp.where(even, in_ref[...], out_ref[...])
+    raw = jnp.concatenate([top, bot], axis=0).reshape(240, C0)
     k_new, v_new = keys_values(raw, gain_ref, wp_ref)
     k_new = k_new.reshape(6, 40, C0)
     v_new = v_new.reshape(6, 40, C0)
@@ -434,8 +452,8 @@
     return jax.ShapeDtypeStruct(shape, F32)
 
 
-def shift(n, step):
-    return [(i, i + step) for i in range(n) if 0 <= i + step < n]
+def odd_swaps(n):
+    return [p for i in range(1, n - 1, 2) for p in ((i, i + 1), (i + 1, i))]
 
 
 V = pl.BlockSpec(memory_space=pltpu.VMEM)
@@ -473,9 +491,9 @@
     global_gain, global_project, global_output, global_scale, split_second, split_first,
 ):
     gain = local_gain[None]
-    first, last = call(edge_kernel, "v", (f32(ROWS, 3, C0), f32(ROWS, 3, C0)))(latent)
-    right = lax.ppermute(first, COL_AXIS, shift(16, -1))
-    left = lax.ppermute(last, COL_AXIS, shift(16, 1))
+    inner, outer = call(edge_kernel, "v", (f32(ROWS, 3, C0), f32(ROWS, 3, C0)))(latent)
+    col_in = lax.ppermute(inner, "c", [(0, 1), (1, 0)])
+    col_out = lax.ppermute(outer, COL_AXIS, odd_swaps(16))
     q, k, v = call(
         own_kernel,
         "vhhh",
@@ -483,23 +501,25 @@
         [(1, C0), (C0, 3 * C0), pltpu.SMEM((HEADS0,), F32), DMA((3,))],
         us=5,
     )(latent, gain, local_project, local_scale)
-    up, down = call(row_kernel, "vvv", (f32(3, 40, C0), f32(3, 40, C0)))(latent, left, right)
-    bot = lax.ppermute(up, ROW_AXIS, shift(8, -1))
-    top = lax.ppermute(down, ROW_AXIS, shift(8, 1))
+    inner, outer = call(row_kernel, "vvv", (f32(3, 40, C0), f32(3, 40, C0)))(
+        latent, col_in, col_out
+    )
+    row_in = lax.ppermute(inner, "xl", [(0, 1), (1, 0)])
+    row_out = lax.ppermute(outer, ROW_AXIS, odd_swaps(8))
     kw, vw, mid = call(
         middle_kernel,
         "v" * 9,
         (f32(2, ROWS, SLOTS, C0), f32(2, ROWS, SLOTS, C0), f32(256, C0)),
         [(ROWS, 8, C0)],
         us=8,
-    )(latent, left, right, q, k, v, gain, local_project, local_output)
+    )(latent, col_in, col_out, q, k, v, gain, local_project, local_output)
     l0, l1, l2, one, nx = call(
         outer_kernel,
         "v" * 13,
         (f32(2, 512, 128), f32(128, CM), f32(32, CG), f32(32, CG), f32(16, 32, CG)),
         [(512, C0)],
     )(
-        latent, top, bot, q, kw, vw, mid, gain, local_project, local_output,
+        latent, row_in, row_out, q, kw, vw, mid, gain, local_project, local_output,
         merge_first, merge_second, global_gain[None],
     )
     keys_from = lax.all_to_all(nx, ZX, 0, 0, tiled=True)

time: 80.2 us -> 75.6 us (0.943)
  starting transfers between devices: 33.4 us -> 27.2 us
  waiting for transfers between devices: 13.6 us -> 15.2 us
    ppermute x4, starting transfers between devices: 11.5 us -> 7.17 us  [the longest x1 4.66 us: shards(): col_out = lax.ppermute(outer, COL_AXIS, odd_swaps(16))]
    all_to_all x1, waiting for transfers between devices: 2 us -> 4.55 us  [shards(): keys_from = lax.all_to_all(nx, ZX, 0, 0, tiled=True)]
    ppermute x1, starting transfers between devices: 2.62 us -> 1.15 us  [shards(): theirs = lax.ppermute(other, 'c', [(0, 1), (1, 0)])]
    ppermute x4, waiting for transfers between devices: 1.17 us -> 0.01 us  [the longest x1 0.01 us: shards(): col_in = lax.ppermute(inner, 'c', [(0, 1), (1, 0)])]
  transfers between devices with their start and end apart: 13 -> 13, of which waited for: 8 -> 6; matrix products, arithmetic and copies ran while one was open for 0% -> 0% of each run, Pallas kernels for 15% -> 16%
where the time goes in v2:
time: 75.6 us; the launch traced here: 74.9 us
  Pallas kernels  29.2 us (39%)
  starting transfers between devices  27.2 us (36%)
  waiting for transfers between devices  15.2 us (20%)
  local copies, waits for them, and re-layouts  3.02 us (4%)
    pallas_call x9, Pallas kernels, placed(): run(*(pltpu.with_memory_space_constraint(a, pltpu.HBM) if i == 'h' else a...  29.2 us
    all_to_all x1, starting transfers between devices, shards(): keys_from = lax.all_to_all(nx, ZX, 0, 0, tiled=True)  10.2 us
    ppermute x3, waiting for transfers between devices, shards(): lax.ppermute(two, 'y', [(i, (i + d) % 4) for i in range(4)])  5.03 us
    ppermute x1, starting transfers between devices, shards(): col_out = lax.ppermute(outer, COL_AXIS, odd_swaps(16))  4.66 us
    all_to_all x1, waiting for transfers between devices, shards(): keys_from = lax.all_to_all(nx, ZX, 0, 0, tiled=True)  4.55 us
    ppermute x3, starting transfers between devices, shards(): lax.ppermute(two, 'y', [(i, (i + d) % 4) for i in range(4)])  4.31 us
    ppermute x3, starting transfers between devices, shards(): lax.ppermute(part, 'y', [(i, (i - d) % 4) for i in range(4)])  4.06 us
    ppermute x3, waiting for transfers between devices, shards(): lax.ppermute(part, 'y', [(i, (i - d) % 4) for i in range(4)])  3.34 us
  transfers between devices with their start and end apart: 13, of which 6 were waited for; matrix products, arithmetic and copies ran while one was open for 0% of the time, Pallas kernels for 16%

profile of v2, /device:TPU:1, one launch (start us, length us, event | category | flops | bytes accessed | tf_op | source)
XLA Modules:
  0.0 74.9 jit_solution(14592251128669806917)
XLA Ops:
  0.0 1.0 %copy-done.7 = f32[16,32,256]{2,1,0:T(8,128)S(1)} copy-done((f32[16,32,256]{2,1,0:T(8,128)S(1)}, f32[16,32,256]{2,1,0:T(8,128)}, u32[]{:S(2)}) %copy-start.7) | copy-done | bytes 524312
  1.1 1.5 %collective-permute-start = (f32[16,3,256]{2,1,0:T(4,128)S(1)}, f32[16,3,256]{2,1,0:T(4,128)S(1)}, u32[]{:S(2)}, u32[]{:S(2)}) collective-permute-start(f32[16,3,256]{2,1,0:T(4,128)S(1)} %get-tuple-element.26), channel_id=1, source_target_pairs={{0,1},{1,0},{2,3},{3,2},{4,5},{5,4},{6,7},{7,6},{8,9},{9,8},{10,11... | collective-permute-start | bytes 147464 | tf_op jit(solution)/shard_map/ppermute | solution.py:495
  2.5 4.7 %collective-permute-start.1 = (f32[16,3,256]{2,1,0:T(4,128)S(1)}, f32[16,3,256]{2,1,0:T(4,128)S(1)}, u32[]{:S(2)}, u32[]{:S(2)}) collective-permute-start(f32[16,3,256]{2,1,0:T(4,128)S(1)} %get-tuple-element.27), channel_id=1, source_target_pairs={{1,2},{2,1},{3,4},{4,3},{5,6},{6,5},{7,8},{8,7},{9,10},{10,9},{11,... | collective-permute-start | bytes 147464 | tf_op jit(solution)/shard_map/ppermute | solution.py:496
  7.2 0.0 copy-start.6
  7.2 0.0 copy-start.8
  7.2 0.0 copy-start.10
  7.2 3.9 %shard_map.129 = (f32[512,256]{1,0:T(8,128)S(1)}, f32[16,32,256]{2,1,0:T(8,128)S(1)}, f32[16,32,256]{2,1,0:T(8,128)S(1)}) custom-call(f32[16,32,256]{2,1,0:T(8,128)S(1)} %copy-done.7, f32[1,256]{1,0:T(1,128)} %bitcast.8, f32[256,768]{1,0:T(8,128)} %wp_ref.3, f32[4]{0:T(128)} %scale_hbm.2), custom_call_target="tpu_custom_call" | custom-call | flops 2000000000 | bytes 1048576 | tf_op jit(solution)/shard_map/pallas_call | solution.py:479
  11.3 0.4 collective-permute-start.2
  11.7 0.7 collective-permute-start.3
  12.4 0.0 copy-start.9
  12.4 5.4 %shard_map.130 = (f32[2,16,24,256]{3,2,1,0:T(8,128)S(1)}, f32[2,16,24,256]{3,2,1,0:T(8,128)S(1)}, f32[256,256]{1,0:T(8,128)S(1)}) custom-call(f32[16,32,256]{2,1,0:T(8,128)S(1)} %copy-done.7, f32[16,3,256]{2,1,0:T(4,128)S(1)} %collective-permute-done.in_ref, f32[16,3,256]{2,1,0:T(4,128)S(1)} %collective-permute-done.1.out_ref, ...), custom_call_target="tpu_custom_call" | custom-call | flops 3200000000 | bytes 1048576 | tf_op jit(solution)/shard_map/pallas_call | solution.py:479
  17.8 7.9 %shard_map.131 = (f32[2,512,128]{2,1,0:T(8,128)S(1)}, f32[128,384]{1,0:T(8,128)S(1)}, f32[32,512]{1,0:T(8,128)S(1)}, f32[32,512]{1,0:T(8,128)S(1)}, f32[16,32,512]{2,1,0:T(8,128)}) custom-call(f32[16,32,256]{2,1,0:T(8,128)S(1)} %copy-done.7, f32[3,40,256]{2,1,0:T(8,128)S(1)} %collective-permute-done.2.in_ref, ...), custom_call_target="tpu_custom_call" | custom-call | flops 400000000 | bytes 1048576 | tf_op jit(solution)/shard_map/pallas_call | solution.py:479
  25.8 10.2 %all-to-all-start = ((f32[16,32,512]{2,1,0:T(8,128)}), f32[16,32,512]{2,1,0:T(8,128)S(1)}, u32[]{:S(2)}, u32[]{:S(2)}) async-start(f32[16,32,512]{2,1,0:T(8,128)} %get-tuple-element.36), calls=%async_computation | async-start | bytes 2097152 | tf_op jit(solution)/shard_map/all_to_all | solution.py:525
  36.0 2.7 %shard_map.132 = f32[32,512]{1,0:T(8,128)S(1)} custom-call(f32[32,512]{1,0:T(8,128)S(1)} %get-tuple-element.37.x_ref, f32[512,1536]{1,0:T(8,128)} %gp_ref.1, f32[8]{0:T(128)} %scale_hbm.3), custom_call_target="tpu_custom_call" | custom-call | flops 1600000000 | bytes 1048576 | tf_op jit(solution)/shard_map/pallas_call | solution.py:479
  38.7 0.3 collective-permute-start.4
  39.0 1.0 %collective-permute-done.4 = f32[32,512]{1,0:T(8,128)S(1)} collective-permute-done((f32[32,512]{1,0:T(8,128)S(1)}, f32[32,512]{1,0:T(8,128)S(1)}, u32[]{:S(2)}, u32[]{:S(2)}) %collective-permute-start.4) | collective-permute-done | bytes 65568 | tf_op jit(solution)/shard_map/ppermute | solution.py:533
  40.0 2.8 %collective-permute-start.7 = (f32[2,32,512]{2,1,0:T(8,128)S(1)}, f32[2,32,512]{2,1,0:T(8,128)S(1)}, u32[]{:S(2)}, u32[]{:S(2)}) collective-permute-start(f32[2,32,512]{2,1,0:T(8,128)S(1)} %pad_maximum_fusion), channel_id=1, source_target_pairs={{0,8},{4,12},{8,0},{12,4},{1,9},{5,13},{9,1},{13,5},{2,10},{6,14},... | collective-permute-start | bytes 393224 | tf_op jit(solution)/shard_map/ppermute | solution.py:535
  42.9 0.9 %collective-permute-start.6 = (f32[2,32,512]{2,1,0:T(8,128)S(1)}, f32[2,32,512]{2,1,0:T(8,128)S(1)}, u32[]{:S(2)}, u32[]{:S(2)}) collective-permute-start(f32[2,32,512]{2,1,0:T(8,128)S(1)} %pad_maximum_fusion), channel_id=1, source_target_pairs={{0,12},{4,0},{8,4},{12,8},{1,13},{5,1},{9,5},{13,9},{2,14},{6,2},{... | collective-permute-start | bytes 393224 | tf_op jit(solution)/shard_map/ppermute | solution.py:535
  43.8 0.5 collective-permute-start.5
  44.3 5.0 %collective-permute-done.5 = f32[2,32,512]{2,1,0:T(8,128)S(1)} collective-permute-done((f32[2,32,512]{2,1,0:T(8,128)S(1)}, f32[2,32,512]{2,1,0:T(8,128)S(1)}, u32[]{:S(2)}, u32[]{:S(2)}) %collective-permute-start.5) | collective-permute-done | bytes 131104 | tf_op jit(solution)/shard_map/ppermute | solution.py:535
  49.4 4.5 %all-to-all-done.x_ref = f32[16,32,512]{2,1,0:T(8,128)S(1)} async-done(((f32[16,32,512]{2,1,0:T(8,128)}), f32[16,32,512]{2,1,0:T(8,128)S(1)}, u32[]{:S(2)}, u32[]{:S(2)}) %all-to-all-start) | async-done | bytes 1048608 | tf_op jit(solution)/shard_map/all_to_all | solution.py:525
  54.0 1.9 %copy-done.1 = f32[512,1536]{1,0:T(8,128)S(1)} copy-done((f32[512,1536]{1,0:T(8,128)S(1)}, f32[512,1536]{1,0:T(8,128)}, u32[]{:S(2)}) %copy-start.1) | copy-done | bytes 3145752
  55.9 5.3 %shard_map.133 = (f32[4,32,640]{2,1,0:T(8,128)S(1)}, f32[4,32,640]{2,1,0:T(8,128)S(1)}) custom-call(f32[16,32,512]{2,1,0:T(8,128)S(1)} %all-to-all-done.x_ref, f32[8,32,512]{2,1,0:T(8,128)S(1)} %constant_dynamic-update-slice_fusion.q_ref, f32[512,1536]{1,0:T(8,128)S(1)} %copy-done.1), custom_call_target="tpu_custom_call" | custom-call | flops 400000000 | bytes 1048576 | tf_op jit(solution)/shard_map/pallas_call | solution.py:479
  61.2 1.1 %collective-permute-start.8 = (f32[4,32,640]{2,1,0:T(8,128)S(1)}, f32[4,32,640]{2,1,0:T(8,128)S(1)}, u32[]{:S(2)}, u32[]{:S(2)}) collective-permute-start(f32[4,32,640]{2,1,0:T(8,128)S(1)} %get-tuple-element.39), channel_id=1, source_target_pairs={{0,1},{1,0},{2,3},{3,2},{4,5},{5,4},{6,7},{7,6},{8,9},{9,8},{10,11... | collective-permute-start | bytes 983048 | tf_op jit(solution)/shard_map/ppermute | solution.py:543
  62.3 1.3 %collective-permute-done.8.b_ref = f32[4,32,640]{2,1,0:T(8,128)S(1)} collective-permute-done((f32[4,32,640]{2,1,0:T(8,128)S(1)}, f32[4,32,640]{2,1,0:T(8,128)S(1)}, u32[]{:S(2)}, u32[]{:S(2)}) %collective-permute-start.8) | collective-permute-done | bytes 327712 | tf_op jit(solution)/shard_map/ppermute | solution.py:543
  63.6 0.6 shard_map.134
  64.2 0.3 collective-permute-start.9
  64.5 1.2 %collective-permute-start.10 = (f32[32,640]{1,0:T(8,128)S(1)}, f32[32,640]{1,0:T(8,128)S(1)}, u32[]{:S(2)}, u32[]{:S(2)}) collective-permute-start(f32[32,640]{1,0:T(8,128)S(1)} %get-tuple-element.42), channel_id=1, source_target_pairs={{0,4},{4,8},{8,12},{12,0},{1,5},{5,9},{9,13},{13,1},{2,6},{6,10},{... | collective-permute-start | bytes 245768 | tf_op jit(solution)/shard_map/ppermute | solution.py:546
  65.7 2.5 %collective-permute-start.11 = (f32[32,640]{1,0:T(8,128)S(1)}, f32[32,640]{1,0:T(8,128)S(1)}, u32[]{:S(2)}, u32[]{:S(2)}) collective-permute-start(f32[32,640]{1,0:T(8,128)S(1)} %get-tuple-element.43), channel_id=1, source_target_pairs={{0,8},{4,12},{8,0},{12,4},{1,9},{5,13},{9,1},{13,5},{2,10},{6,14},... | collective-permute-start | bytes 245768 | tf_op jit(solution)/shard_map/ppermute | solution.py:546
  68.2 0.7 collective-permute-done.10.p2_ref
  69.0 2.6 %collective-permute-done.11.p3_ref = f32[32,640]{1,0:T(8,128)S(1)} collective-permute-done((f32[32,640]{1,0:T(8,128)S(1)}, f32[32,640]{1,0:T(8,128)S(1)}, u32[]{:S(2)}, u32[]{:S(2)}) %collective-permute-start.11) | collective-permute-done | bytes 81952 | tf_op jit(solution)/shard_map/ppermute | solution.py:546
  71.6 3.3 %shard_map.135 = f32[16,32,256]{2,1,0:T(8,128)} custom-call(f32[32,640]{1,0:T(8,128)S(1)} %get-tuple-element.40.p0_ref, f32[32,640]{1,0:T(8,128)S(1)} %collective-permute-done.9.p1_ref, f32[32,640]{1,0:T(8,128)S(1)} %collective-permute-done.10.p2_ref, f32[32,640]{1,0:T(8,128)S(1)} %collective-permute-done.11.p3_ref, ...), custom_call_target="tpu_custom_call" | custom-call | flops 400000000 | bytes 1048576 | tf_op jit(solution)/shard_map/pallas_call | solution.py:479
  (31 shorter events, 0.2 us)
Async XLA Ops:
  0.0 1.0 %copy-start.7 = (f32[16,32,256]{2,1,0:T(8,128)S(1)}, f32[16,32,256]{2,1,0:T(8,128)}, u32[]{:S(2)}) copy-start(f32[16,32,256]{2,1,0:T(8,128)} %x_ref.9) | copy-start | bytes 1572868
  1.1 10.1 %collective-permute-start = (f32[16,3,256]{2,1,0:T(4,128)S(1)}, f32[16,3,256]{2,1,0:T(4,128)S(1)}, u32[]{:S(2)}, u32[]{:S(2)}) collective-permute-start(f32[16,3,256]{2,1,0:T(4,128)S(1)} %get-tuple-element.26), channel_id=1, source_target_pairs={{0,1},{1,0},{2,3},{3,2},{4,5},{5,4},{6,7},{7,6},{8,9},{9,8},{10,11... | collective-permute-start | bytes 147464 | tf_op jit(solution)/shard_map/ppermute | solution.py:495
  2.5 8.7 %collective-permute-start.1 = (f32[16,3,256]{2,1,0:T(4,128)S(1)}, f32[16,3,256]{2,1,0:T(4,128)S(1)}, u32[]{:S(2)}, u32[]{:S(2)}) collective-permute-start(f32[16,3,256]{2,1,0:T(4,128)S(1)} %get-tuple-element.27), channel_id=1, source_target_pairs={{1,2},{2,1},{3,4},{4,3},{5,6},{6,5},{7,8},{8,7},{9,10},{10,9},{11,... | collective-permute-start | bytes 147464 | tf_op jit(solution)/shard_map/ppermute | solution.py:496
  7.2 5.1 %copy-start.6 = (f32[256,768]{1,0:T(8,128)S(1)}, f32[256,768]{1,0:T(8,128)}, u32[]{:S(2)}) copy-start(f32[256,768]{1,0:T(8,128)} %wp_ref.3) | copy-start | bytes 2359300
  7.2 5.1 %copy-start.8 = (f32[256,256]{1,0:T(8,128)S(1)}, f32[256,256]{1,0:T(8,128)}, u32[]{:S(2)}) copy-start(f32[256,256]{1,0:T(8,128)} %wo_ref.3) | copy-start | bytes 786436
  7.2 5.1 %copy-start.10 = (f32[256]{0:T(256)S(1)}, f32[256]{0:T(256)}, u32[]{:S(2)}) copy-start(f32[256]{0:T(256)} %param.14) | copy-start | bytes 3076
  11.3 6.5 %collective-permute-start.2 = (f32[3,40,256]{2,1,0:T(8,128)S(1)}, f32[3,40,256]{2,1,0:T(8,128)S(1)}, u32[]{:S(2)}, u32[]{:S(2)}) collective-permute-start(f32[3,40,256]{2,1,0:T(8,128)S(1)} %get-tuple-element.28), channel_id=1, source_target_pairs={{0,16},{16,0},{1,17},{17,1},{2,18},{18,2},{3,19},{19,3},{4,20},{20... | collective-permute-start | bytes 368648 | tf_op jit(solution)/shard_map/ppermute | solution.py:507
  11.7 6.1 %collective-permute-start.3 = (f32[3,40,256]{2,1,0:T(8,128)S(1)}, f32[3,40,256]{2,1,0:T(8,128)S(1)}, u32[]{:S(2)}, u32[]{:S(2)}) collective-permute-start(f32[3,40,256]{2,1,0:T(8,128)S(1)} %get-tuple-element.29), channel_id=1, source_target_pairs={{16,32},{32,16},{48,64},{64,48},{80,96},{96,80},{17,33},{33,17},{4... | collective-permute-start | bytes 368648 | tf_op jit(solution)/shard_map/ppermute | solution.py:508
  12.3 5.5 %copy-start.2 = (f32[1536,512]{1,0:T(8,128)S(1)}, f32[1536,512]{1,0:T(8,128)}, u32[]{:S(2)}) copy-start(f32[1536,512]{1,0:T(8,128)} %m2_ref.1) | copy-start | bytes 9437188
  12.4 5.5 %copy-start.4 = (f32[1024,384]{1,0:T(8,128)S(1)}, f32[1024,384]{1,0:T(8,128)}, u32[]{:S(2)}) copy-start(f32[1024,384]{1,0:T(8,128)} %m1_ref.1) | copy-start | bytes 4718596
  12.4 5.5 %copy-start.9 = (f32[512]{0:T(512)S(1)}, f32[512]{0:T(512)}, u32[]{:S(2)}) copy-start(f32[512]{0:T(512)} %param.20) | copy-start | bytes 6148
  25.8 28.2 %all-to-all-start = ((f32[16,32,512]{2,1,0:T(8,128)}), f32[16,32,512]{2,1,0:T(8,128)S(1)}, u32[]{:S(2)}, u32[]{:S(2)}) async-start(f32[16,32,512]{2,1,0:T(8,128)} %get-tuple-element.36), calls=%async_computation | async-start | bytes 2097152 | tf_op jit(solution)/shard_map/all_to_all | solution.py:525
  38.7 1.3 %collective-permute-start.4 = (f32[32,512]{1,0:T(8,128)S(1)}, f32[32,512]{1,0:T(8,128)S(1)}, u32[]{:S(2)}, u32[]{:S(2)}) collective-permute-start(f32[32,512]{1,0:T(8,128)S(1)} %shard_map.132), channel_id=1, source_target_pairs={{0,1},{1,0},{2,3},{3,2},{4,5},{5,4},{6,7},{7,6},{8,9},{9,8},{10,11... | collective-permute-start | bytes 196616 | tf_op jit(solution)/shard_map/ppermute | solution.py:533
  40.0 9.4 %collective-permute-start.7 = (f32[2,32,512]{2,1,0:T(8,128)S(1)}, f32[2,32,512]{2,1,0:T(8,128)S(1)}, u32[]{:S(2)}, u32[]{:S(2)}) collective-permute-start(f32[2,32,512]{2,1,0:T(8,128)S(1)} %pad_maximum_fusion), channel_id=1, source_target_pairs={{0,8},{4,12},{8,0},{12,4},{1,9},{5,13},{9,1},{13,5},{2,10},{6,14},... | collective-permute-start | bytes 393224 | tf_op jit(solution)/shard_map/ppermute | solution.py:535
  42.9 6.5 %collective-permute-start.6 = (f32[2,32,512]{2,1,0:T(8,128)S(1)}, f32[2,32,512]{2,1,0:T(8,128)S(1)}, u32[]{:S(2)}, u32[]{:S(2)}) collective-permute-start(f32[2,32,512]{2,1,0:T(8,128)S(1)} %pad_maximum_fusion), channel_id=1, source_target_pairs={{0,12},{4,0},{8,4},{12,8},{1,13},{5,1},{9,5},{13,9},{2,14},{6,2},{... | collective-permute-start | bytes 393224 | tf_op jit(solution)/shard_map/ppermute | solution.py:535
  43.8 5.6 %collective-permute-start.5 = (f32[2,32,512]{2,1,0:T(8,128)S(1)}, f32[2,32,512]{2,1,0:T(8,128)S(1)}, u32[]{:S(2)}, u32[]{:S(2)}) collective-permute-start(f32[2,32,512]{2,1,0:T(8,128)S(1)} %pad_maximum_fusion), channel_id=1, source_target_pairs={{0,4},{4,8},{8,12},{12,0},{1,5},{5,9},{9,13},{13,1},{2,6},{6,10},{... | collective-permute-start | bytes 393224 | tf_op jit(solution)/shard_map/ppermute | solution.py:535
  54.0 1.9 %copy-start.1 = (f32[512,1536]{1,0:T(8,128)S(1)}, f32[512,1536]{1,0:T(8,128)}, u32[]{:S(2)}) copy-start(f32[512,1536]{1,0:T(8,128)} %gp_ref.1) | copy-start | bytes 9437188
  55.9 15.7 %copy-start = (f32[512,1536]{1,0:T(8,128)S(1)}, f32[512,1536]{1,0:T(8,128)}, u32[]{:S(2)}) copy-start(f32[512,1536]{1,0:T(8,128)} %s2_ref.1) | copy-start | bytes 9437188
  55.9 15.7 %copy-start.3 = (f32[384,1024]{1,0:T(8,128)S(1)}, f32[384,1024]{1,0:T(8,128)}, u32[]{:S(2)}) copy-start(f32[384,1024]{1,0:T(8,128)} %s1_ref.1) | copy-start | bytes 4718596
  55.9 15.7 %copy-start.5 = (f32[512,512]{1,0:T(8,128)S(1)}, f32[512,512]{1,0:T(8,128)}, u32[]{:S(2)}) copy-start(f32[512,512]{1,0:T(8,128)} %go_ref.1) | copy-start | bytes 3145732
  61.2 2.4 %collective-permute-start.8 = (f32[4,32,640]{2,1,0:T(8,128)S(1)}, f32[4,32,640]{2,1,0:T(8,128)S(1)}, u32[]{:S(2)}, u32[]{:S(2)}) collective-permute-start(f32[4,32,640]{2,1,0:T(8,128)S(1)} %get-tuple-element.39), channel_id=1, source_target_pairs={{0,1},{1,0},{2,3},{3,2},{4,5},{5,4},{6,7},{7,6},{8,9},{9,8},{10,11... | collective-permute-start | bytes 983048 | tf_op jit(solution)/shard_map/ppermute | solution.py:543
  64.2 4.1 %collective-permute-start.9 = (f32[32,640]{1,0:T(8,128)S(1)}, f32[32,640]{1,0:T(8,128)S(1)}, u32[]{:S(2)}, u32[]{:S(2)}) collective-permute-start(f32[32,640]{1,0:T(8,128)S(1)} %get-tuple-element.41), channel_id=1, source_target_pairs={{0,12},{4,0},{8,4},{12,8},{1,13},{5,1},{9,5},{13,9},{2,14},{6,2},{... | collective-permute-start | bytes 245768 | tf_op jit(solution)/shard_map/ppermute | solution.py:546
  64.5 4.5 %collective-permute-start.10 = (f32[32,640]{1,0:T(8,128)S(1)}, f32[32,640]{1,0:T(8,128)S(1)}, u32[]{:S(2)}, u32[]{:S(2)}) collective-permute-start(f32[32,640]{1,0:T(8,128)S(1)} %get-tuple-element.42), channel_id=1, source_target_pairs={{0,4},{4,8},{8,12},{12,0},{1,5},{5,9},{9,13},{13,1},{2,6},{6,10},{... | collective-permute-start | bytes 245768 | tf_op jit(solution)/shard_map/ppermute | solution.py:546
  65.7 5.9 %collective-permute-start.11 = (f32[32,640]{1,0:T(8,128)S(1)}, f32[32,640]{1,0:T(8,128)S(1)}, u32[]{:S(2)}, u32[]{:S(2)}) collective-permute-start(f32[32,640]{1,0:T(8,128)S(1)} %get-tuple-element.43), channel_id=1, source_target_pairs={{0,8},{4,12},{8,0},{12,4},{1,9},{5,13},{9,1},{13,5},{2,10},{6,14},... | collective-permute-start | bytes 245768 | tf_op jit(solution)/shard_map/ppermute | solution.py:546

commit v3 on v2

--- a/solution.py
+++ b/solution.py
@@ -30,7 +30,6 @@
 F32 = jnp.float32
 ROW_AXIS = ("z", "xl")
 COL_AXIS = ("y", "xh", "c")
-ZX = ("z", "xh", "xl")
 TURNS = (1, 3, 2)
 CLASSES = [(a1, b1, a2, b2) for a1 in (0, 1) for b1 in (0, 1) for a2 in (0, 1) for b2 in (0, 1)]
 
@@ -261,7 +260,7 @@
 def outer_kernel(
     x_ref, in_ref, out_ref, q_ref, kw_ref, vw_ref, mid_ref, gain_ref, wp_ref, wo_ref,
     m1_ref, m2_ref, ggain_ref,
-    l0_ref, l1_ref, l2_ref, one_ref, nx_ref, order,
+    l0_ref, l1_ref, l2_ref, one_ref, order,
 ):
     even = lax.axis_index("xl") == 0
     top = jnp.where(even, out_ref[...], in_ref[...])
@@ -314,10 +313,7 @@
     for n in range(1, 4):
         two = two + mm(one[n * 32 : (n + 1) * 32], m2_ref[n * CM : (n + 1) * CM, :])
     l2_ref[...] = two
-    normed_two = rms(two, ggain_ref[...])
-    one_ref[...] = normed_two
-    for n in range(16):
-        nx_ref[n] = normed_two
+    one_ref[...] = rms(two, ggain_ref[...])
 
 
 def chunks_in(gp_hbm, weight, sems, width):
@@ -357,9 +353,9 @@
     return jnp.concatenate(tiles, axis=1)
 
 
-def attention_kernel(x_ref, q_ref, gp_ref, mine_ref, other_ref, kk, vv):
+def attention_kernel(x0_ref, x1_ref, x2_ref, x3_ref, q_ref, gp_ref, mine_ref, other_ref, kk, vv):
     first = iota((1, 128), 1) < HEAD
-    x = x_ref[...].reshape(512, CG)
+    x = jnp.concatenate([ref[...] for ref in (x0_ref, x1_ref, x2_ref, x3_ref)], axis=0)
     kk[...] = floored(mm(x, picked(gp_ref, 2, 0, first)))
     vv[...] = mm(x, picked(gp_ref, 1, 2, first))
     lane = iota((256, 128), 1)
@@ -452,6 +448,10 @@
     return jax.ShapeDtypeStruct(shape, F32)
 
 
+def swaps(value, axis):
+    return [lax.ppermute(value, axis, [(i, i ^ d) for i in range(4)]) for d in TURNS]
+
+
 def odd_swaps(n):
     return [p for i in range(1, n - 1, 2) for p in ((i, i + 1), (i + 1, i))]
 
@@ -513,16 +513,16 @@
         [(ROWS, 8, C0)],
         us=8,
     )(latent, col_in, col_out, q, k, v, gain, local_project, local_output)
-    l0, l1, l2, one, nx = call(
+    l0, l1, l2, one = call(
         outer_kernel,
         "v" * 13,
-        (f32(2, 512, 128), f32(128, CM), f32(32, CG), f32(32, CG), f32(16, 32, CG)),
+        (f32(2, 512, 128), f32(128, CM), f32(32, CG), f32(32, CG)),
         [(512, C0)],
     )(
         latent, row_in, row_out, q, kw, vw, mid, gain, local_project, local_output,
         merge_first, merge_second, global_gain[None],
     )
-    keys_from = lax.all_to_all(nx, ZX, 0, 0, tiled=True)
+    moved = swaps(one, ("xl", "xh"))
     qg = call(
         query_kernel,
         "vhh",
@@ -530,20 +530,21 @@
         [(CG, 3 * CG), pltpu.SMEM((HEADS_G,), F32), DMA((5,))],
         us=4,
     )(one, global_project, global_scale)
+    row = jnp.concatenate([one] + moved)
+    keys_from = [row] + swaps(row, "z")
     swapped = lax.ppermute(qg, "c", [(0, 1), (1, 0)])
     two = jnp.stack([qg, swapped])
-    around = [lax.ppermute(two, "y", [(i, (i + d) % 4) for i in range(4)]) for d in TURNS]
-    queries_from = jnp.concatenate([two] + around)
+    queries_from = jnp.concatenate([two] + swaps(two, "y"))
     mine, other = call(
         attention_kernel,
-        "vvv",
+        "vvvvvv",
         (f32(4, 32, CG + 128), f32(4, 32, CG + 128)),
         [(512, CG), (512, CG)],
-    )(keys_from, queries_from, global_project)
+    )(*keys_from, queries_from, global_project)
     theirs = lax.ppermute(other, "c", [(0, 1), (1, 0)])
     merged = call(merge_kernel, "vv", tuple(f32(32, CG + 128) for _ in range(4)))(mine, theirs)
     arrived = [merged[0]] + [
-        lax.ppermute(part, "y", [(i, (i - d) % 4) for i in range(4)])
+        lax.ppermute(part, "y", [(i, i ^ d) for i in range(4)])
         for part, d in zip(merged[1:], TURNS)
     ]
     return call(tail_kernel, "v" * 10, f32(ROWS, COLS, C0), [(2, 512, 128)])(

time: 75.6 us -> 75.9 us (level)
  starting transfers between devices: 27.2 us -> 29.6 us
  local copies, waits for them, and re-layouts: 3.02 us -> 1.17 us
  Pallas kernels: 29.2 us -> 28.3 us
    ppermute x6 -> x12, starting transfers between devices: 8.37 us -> 19.7 us  [the longest x9 16.4 us: swaps(): lax.ppermute(value, axis, [(i, i ^ d) for i in range(4)])]
    all_to_all x1 -> x0, starting transfers between devices: 10.2 us -> none  [shards(): keys_from = lax.all_to_all(nx, ZX, 0, 0, tiled=True)]
    ppermute x6 -> x12, waiting for transfers between devices: 8.38 us -> 14.2 us  [the longest x9 10.4 us: swaps(): lax.ppermute(value, axis, [(i, i ^ d) for i in range(4)])]
    all_to_all x1 -> x0, waiting for transfers between devices: 4.55 us -> none  [shards(): keys_from = lax.all_to_all(nx, ZX, 0, 0, tiled=True)]
    unnamed x26 -> x29, local copies, waits for them, and re-layouts: 3.01 us -> 1.16 us
    ppermute x1, starting transfers between devices: 1.15 us -> 2.43 us  [shards(): theirs = lax.ppermute(other, 'c', [(0, 1), (1, 0)])]
    ppermute x1, waiting for transfers between devices: 1.04 us -> 0.01 us  [shards(): swapped = lax.ppermute(qg, 'c', [(0, 1), (1, 0)])]
    pallas_call x9, Pallas kernels: 29.2 us -> 28.3 us  [placed(): run(*(pltpu.with_memory_space_constraint(a, pltpu.HBM) if i == 'h' else a...]
  transfers between devices with their start and end apart: 13 -> 18, of which waited for: 6 -> 8; matrix products, arithmetic and copies ran while one was open for 0% -> 0% of each run, Pallas kernels for 16% -> 12%
where the time goes in v3:
time: 75.9 us; the launch traced here: 74.9 us
  starting transfers between devices  29.6 us (39%)
  Pallas kernels  28.3 us (37%)
  waiting for transfers between devices  15.5 us (20%)
  local copies, waits for them, and re-layouts  1.17 us (2%)
    pallas_call x9, Pallas kernels, placed(): run(*(pltpu.with_memory_space_constraint(a, pltpu.HBM) if i == 'h' else a...  28.3 us
    ppermute x9, starting transfers between devices, swaps(): lax.ppermute(value, axis, [(i, i ^ d) for i in range(4)])  16.4 us
    ppermute x9, waiting for transfers between devices, swaps(): lax.ppermute(value, axis, [(i, i ^ d) for i in range(4)])  10.4 us
    ppermute x1, starting transfers between devices, shards(): col_out = lax.ppermute(outer, COL_AXIS, odd_swaps(16))  4.66 us
    ppermute x3, waiting for transfers between devices, shards(): lax.ppermute(part, 'y', [(i, i ^ d) for i in range(4)])  3.76 us
    ppermute x3, starting transfers between devices, shards(): lax.ppermute(part, 'y', [(i, i ^ d) for i in range(4)])  3.33 us
    ppermute x1, starting transfers between devices, shards(): theirs = lax.ppermute(other, 'c', [(0, 1), (1, 0)])  2.43 us
  transfers between devices with their start and end apart: 18, of which 8 were waited for; matrix products, arithmetic and copies ran while one was open for 0% of the time, Pallas kernels for 12%

profile of v3, /device:TPU:1, one launch (start us, length us, event | category | flops | bytes accessed | tf_op | source)
XLA Modules:
  0.0 74.9 jit_solution(4554893229462055095)
XLA Ops:
  0.0 1.0 %copy-done.7 = f32[16,32,256]{2,1,0:T(8,128)S(1)} copy-done((f32[16,32,256]{2,1,0:T(8,128)S(1)}, f32[16,32,256]{2,1,0:T(8,128)}, u32[]{:S(2)}) %copy-start.7) | copy-done | bytes 524312
  1.1 1.5 %collective-permute-start = (f32[16,3,256]{2,1,0:T(4,128)S(1)}, f32[16,3,256]{2,1,0:T(4,128)S(1)}, u32[]{:S(2)}, u32[]{:S(2)}) collective-permute-start(f32[16,3,256]{2,1,0:T(4,128)S(1)} %get-tuple-element.25), channel_id=1, source_target_pairs={{0,1},{1,0},{2,3},{3,2},{4,5},{5,4},{6,7},{7,6},{8,9},{9,8},{10,11... | collective-permute-start | bytes 147464 | tf_op jit(solution)/shard_map/ppermute | solution.py:495
  2.5 4.7 %collective-permute-start.1 = (f32[16,3,256]{2,1,0:T(4,128)S(1)}, f32[16,3,256]{2,1,0:T(4,128)S(1)}, u32[]{:S(2)}, u32[]{:S(2)}) collective-permute-start(f32[16,3,256]{2,1,0:T(4,128)S(1)} %get-tuple-element.26), channel_id=1, source_target_pairs={{1,2},{2,1},{3,4},{4,3},{5,6},{6,5},{7,8},{8,7},{9,10},{10,9},{11,... | collective-permute-start | bytes 147464 | tf_op jit(solution)/shard_map/ppermute | solution.py:496
  7.2 3.9 %shard_map.129 = (f32[512,256]{1,0:T(8,128)S(1)}, f32[16,32,256]{2,1,0:T(8,128)S(1)}, f32[16,32,256]{2,1,0:T(8,128)S(1)}) custom-call(f32[16,32,256]{2,1,0:T(8,128)S(1)} %copy-done.7, f32[1,256]{1,0:T(1,128)} %bitcast.8, f32[256,768]{1,0:T(8,128)} %wp_ref.3, f32[4]{0:T(128)} %scale_hbm.2), custom_call_target="tpu_custom_call" | custom-call | flops 2000000000 | bytes 1048576 | tf_op jit(solution)/shard_map/pallas_call | solution.py:479
  11.3 0.4 collective-permute-start.2
  11.7 0.8 %collective-permute-start.3 = (f32[3,40,256]{2,1,0:T(8,128)S(1)}, f32[3,40,256]{2,1,0:T(8,128)S(1)}, u32[]{:S(2)}, u32[]{:S(2)}) collective-permute-start(f32[3,40,256]{2,1,0:T(8,128)S(1)} %get-tuple-element.28), channel_id=1, source_target_pairs={{16,32},{32,16},{48,64},{64,48},{80,96},{96,80},{17,33},{33,17},{4... | collective-permute-start | bytes 368648 | tf_op jit(solution)/shard_map/ppermute | solution.py:508
  12.6 5.4 %shard_map.130 = (f32[2,16,24,256]{3,2,1,0:T(8,128)S(1)}, f32[2,16,24,256]{3,2,1,0:T(8,128)S(1)}, f32[256,256]{1,0:T(8,128)S(1)}) custom-call(f32[16,32,256]{2,1,0:T(8,128)S(1)} %copy-done.7, f32[16,3,256]{2,1,0:T(4,128)S(1)} %collective-permute-done.in_ref, f32[16,3,256]{2,1,0:T(4,128)S(1)} %collective-permute-done.1.out_ref, ...), custom_call_target="tpu_custom_call" | custom-call | flops 3200000000 | bytes 1048576 | tf_op jit(solution)/shard_map/pallas_call | solution.py:479
  18.0 6.9 %shard_map.131 = (f32[2,512,128]{2,1,0:T(8,128)S(1)}, f32[128,384]{1,0:T(8,128)S(1)}, f32[32,512]{1,0:T(8,128)S(1)}, f32[32,512]{1,0:T(8,128)S(1)}) custom-call(f32[16,32,256]{2,1,0:T(8,128)S(1)} %copy-done.7, f32[3,40,256]{2,1,0:T(8,128)S(1)} %collective-permute-done.2.in_ref, f32[3,40,256]{2,1,0:T(8,128)S(1)} %collective-permute-done.3.out_ref, ...), custom_call_target="tpu_custom_call" | custom-call | flops 400000000 | bytes 1048576 | tf_op jit(solution)/shard_map/pallas_call | solution.py:479
  24.9 2.8 %shard_map.132 = f32[32,512]{1,0:T(8,128)S(1)} custom-call(f32[32,512]{1,0:T(8,128)S(1)} %get-tuple-element.35.x_ref, f32[512,1536]{1,0:T(8,128)} %gp_ref.1, f32[8]{0:T(128)} %scale_hbm.3), custom_call_target="tpu_custom_call" | custom-call | flops 1600000000 | bytes 1048576 | tf_op jit(solution)/shard_map/pallas_call | solution.py:479
  27.9 3.0 %collective-permute-start.4 = (f32[32,512]{1,0:T(8,128)S(1)}, f32[32,512]{1,0:T(8,128)S(1)}, u32[]{:S(2)}, u32[]{:S(2)}) collective-permute-start(f32[32,512]{1,0:T(8,128)S(1)} %get-tuple-element.35.x_ref), channel_id=1, source_target_pairs={{0,2},{2,0},{16,18},{18,16},{1,3},{3,1},{17,19},{19,17},{4,6},{6,4... | collective-permute-start | bytes 196616 | tf_op jit(solution)/shard_map/ppermute | solution.py:452
  30.9 3.5 %collective-permute-start.5 = (f32[32,512]{1,0:T(8,128)S(1)}, f32[32,512]{1,0:T(8,128)S(1)}, u32[]{:S(2)}, u32[]{:S(2)}) collective-permute-start(f32[32,512]{1,0:T(8,128)S(1)} %get-tuple-element.35.x_ref), channel_id=1, source_target_pairs={{0,18},{2,16},{16,2},{18,0},{1,19},{3,17},{17,3},{19,1},{4,22},{6,... | collective-permute-start | bytes 196616 | tf_op jit(solution)/shard_map/ppermute | solution.py:452
  34.4 2.5 %collective-permute-start.11 = (f32[2,32,512]{2,1,0:T(8,128)S(1)}, f32[2,32,512]{2,1,0:T(8,128)S(1)}, u32[]{:S(2)}, u32[]{:S(2)}) collective-permute-start(f32[2,32,512]{2,1,0:T(8,128)S(1)} %pad_maximum_fusion), channel_id=1, source_target_pairs={{0,4},{4,0},{8,12},{12,8},{1,5},{5,1},{9,13},{13,9},{2,6},{6,2},{1... | collective-permute-start | bytes 393224 | tf_op jit(solution)/shard_map/ppermute | solution.py:452
  37.0 1.9 %collective-permute-start.12 = (f32[2,32,512]{2,1,0:T(8,128)S(1)}, f32[2,32,512]{2,1,0:T(8,128)S(1)}, u32[]{:S(2)}, u32[]{:S(2)}) collective-permute-start(f32[2,32,512]{2,1,0:T(8,128)S(1)} %pad_maximum_fusion), channel_id=1, source_target_pairs={{0,12},{4,8},{8,4},{12,0},{1,13},{5,9},{9,5},{13,1},{2,14},{6,10},... | collective-permute-start | bytes 393224 | tf_op jit(solution)/shard_map/ppermute | solution.py:452
  38.9 1.0 %collective-permute-start.13 = (f32[2,32,512]{2,1,0:T(8,128)S(1)}, f32[2,32,512]{2,1,0:T(8,128)S(1)}, u32[]{:S(2)}, u32[]{:S(2)}) collective-permute-start(f32[2,32,512]{2,1,0:T(8,128)S(1)} %pad_maximum_fusion), channel_id=1, source_target_pairs={{0,8},{4,12},{8,0},{12,4},{1,9},{5,13},{9,1},{13,5},{2,10},{6,14},... | collective-permute-start | bytes 393224 | tf_op jit(solution)/shard_map/ppermute | solution.py:452
  39.9 1.7 %collective-permute-start.7 = (f32[128,512]{1,0:T(8,128)S(1)}, f32[128,512]{1,0:T(8,128)S(1)}, u32[]{:S(2)}, u32[]{:S(2)}) collective-permute-start(f32[128,512]{1,0:T(8,128)S(1)} %constant_dynamic-update-slice_fusion.x0_ref), channel_id=1, source_target_pairs={{0,32},{32,0},{64,96},{96,64},{1,33},{33,1},{65,97},{97,65},{2,34}... | collective-permute-start | bytes 786440 | tf_op jit(solution)/shard_map/ppermute | solution.py:452
  41.7 1.9 %collective-permute-start.8 = (f32[128,512]{1,0:T(8,128)S(1)}, f32[128,512]{1,0:T(8,128)S(1)}, u32[]{:S(2)}, u32[]{:S(2)}) collective-permute-start(f32[128,512]{1,0:T(8,128)S(1)} %constant_dynamic-update-slice_fusion.x0_ref), channel_id=1, source_target_pairs={{0,96},{32,64},{64,32},{96,0},{1,97},{33,65},{65,33},{97,1},{2,98}... | collective-permute-start | bytes 786440 | tf_op jit(solution)/shard_map/ppermute | solution.py:452
  43.6 0.8 %collective-permute-start.9 = (f32[128,512]{1,0:T(8,128)S(1)}, f32[128,512]{1,0:T(8,128)S(1)}, u32[]{:S(2)}, u32[]{:S(2)}) collective-permute-start(f32[128,512]{1,0:T(8,128)S(1)} %constant_dynamic-update-slice_fusion.x0_ref), channel_id=1, source_target_pairs={{0,64},{32,96},{64,0},{96,32},{1,65},{33,97},{65,1},{97,33},{2,66}... | collective-permute-start | bytes 786440 | tf_op jit(solution)/shard_map/ppermute | solution.py:452
  44.4 1.5 %collective-permute-done.13 = f32[2,32,512]{2,1,0:T(8,128)S(1)} collective-permute-done((f32[2,32,512]{2,1,0:T(8,128)S(1)}, f32[2,32,512]{2,1,0:T(8,128)S(1)}, u32[]{:S(2)}, u32[]{:S(2)}) %collective-permute-start.13) | collective-permute-done | bytes 131104 | tf_op jit(solution)/shard_map/ppermute | solution.py:452
  45.9 1.1 %collective-permute-done.7.x1_ref = f32[128,512]{1,0:T(8,128)S(1)} collective-permute-done((f32[128,512]{1,0:T(8,128)S(1)}, f32[128,512]{1,0:T(8,128)S(1)}, u32[]{:S(2)}, u32[]{:S(2)}) %collective-permute-start.7) | collective-permute-done | bytes 262176 | tf_op jit(solution)/shard_map/ppermute | solution.py:452
  47.0 2.2 %collective-permute-done.8.x2_ref = f32[128,512]{1,0:T(8,128)S(1)} collective-permute-done((f32[128,512]{1,0:T(8,128)S(1)}, f32[128,512]{1,0:T(8,128)S(1)}, u32[]{:S(2)}, u32[]{:S(2)}) %collective-permute-start.8) | collective-permute-done | bytes 262176 | tf_op jit(solution)/shard_map/ppermute | solution.py:452
  49.2 5.6 %collective-permute-done.9.x3_ref = f32[128,512]{1,0:T(8,128)S(1)} collective-permute-done((f32[128,512]{1,0:T(8,128)S(1)}, f32[128,512]{1,0:T(8,128)S(1)}, u32[]{:S(2)}, u32[]{:S(2)}) %collective-permute-start.9) | collective-permute-done | bytes 262176 | tf_op jit(solution)/shard_map/ppermute | solution.py:452
  54.9 5.3 %shard_map.133 = (f32[4,32,640]{2,1,0:T(8,128)S(1)}, f32[4,32,640]{2,1,0:T(8,128)S(1)}) custom-call(f32[128,512]{1,0:T(8,128)S(1)} %constant_dynamic-update-slice_fusion.x0_ref, f32[128,512]{1,0:T(8,128)S(1)} %collective-permute-done.7.x1_ref, f32[128,512]{1,0:T(8,128)S(1)} %collective-permute-done.8.x2_ref, f32[128,512]{1,0:T(8,128)S(1)} %collective-permute-done.9.x3_ref, ...), custom_call_target="tpu_custom_call" | custom-call | flops 400000000 | bytes 1048576 | tf_op jit(solution)/shard_map/pallas_call | solution.py:479
  60.2 2.4 %collective-permute-start.14 = (f32[4,32,640]{2,1,0:T(8,128)S(1)}, f32[4,32,640]{2,1,0:T(8,128)S(1)}, u32[]{:S(2)}, u32[]{:S(2)}) collective-permute-start(f32[4,32,640]{2,1,0:T(8,128)S(1)} %get-tuple-element.37), channel_id=1, source_target_pairs={{0,1},{1,0},{2,3},{3,2},{4,5},{5,4},{6,7},{7,6},{8,9},{9,8},{10,11... | collective-permute-start | bytes 983048 | tf_op jit(solution)/shard_map/ppermute | solution.py:544
  62.6 1.3 %collective-permute-done.14.b_ref = f32[4,32,640]{2,1,0:T(8,128)S(1)} collective-permute-done((f32[4,32,640]{2,1,0:T(8,128)S(1)}, f32[4,32,640]{2,1,0:T(8,128)S(1)}, u32[]{:S(2)}, u32[]{:S(2)}) %collective-permute-start.14) | collective-permute-done | bytes 327712 | tf_op jit(solution)/shard_map/ppermute | solution.py:544
  63.9 0.6 shard_map.134
  64.5 0.5 collective-permute-start.15
  64.9 1.8 %collective-permute-start.16 = (f32[32,640]{1,0:T(8,128)S(1)}, f32[32,640]{1,0:T(8,128)S(1)}, u32[]{:S(2)}, u32[]{:S(2)}) collective-permute-start(f32[32,640]{1,0:T(8,128)S(1)} %get-tuple-element.40), channel_id=1, source_target_pairs={{0,12},{4,8},{8,4},{12,0},{1,13},{5,9},{9,5},{13,1},{2,14},{6,10},... | collective-permute-start | bytes 245768 | tf_op jit(solution)/shard_map/ppermute | solution.py:547
  66.8 1.0 %collective-permute-start.17 = (f32[32,640]{1,0:T(8,128)S(1)}, f32[32,640]{1,0:T(8,128)S(1)}, u32[]{:S(2)}, u32[]{:S(2)}) collective-permute-start(f32[32,640]{1,0:T(8,128)S(1)} %get-tuple-element.41), channel_id=1, source_target_pairs={{0,8},{4,12},{8,0},{12,4},{1,9},{5,13},{9,1},{13,5},{2,10},{6,14},... | collective-permute-start | bytes 245768 | tf_op jit(solution)/shard_map/ppermute | solution.py:547
  67.8 0.4 collective-permute-done.15.p1_ref
  68.2 1.3 %collective-permute-done.16.p2_ref = f32[32,640]{1,0:T(8,128)S(1)} collective-permute-done((f32[32,640]{1,0:T(8,128)S(1)}, f32[32,640]{1,0:T(8,128)S(1)}, u32[]{:S(2)}, u32[]{:S(2)}) %collective-permute-start.16) | collective-permute-done | bytes 81952 | tf_op jit(solution)/shard_map/ppermute | solution.py:547
  69.5 2.1 %collective-permute-done.17.p3_ref = f32[32,640]{1,0:T(8,128)S(1)} collective-permute-done((f32[32,640]{1,0:T(8,128)S(1)}, f32[32,640]{1,0:T(8,128)S(1)}, u32[]{:S(2)}, u32[]{:S(2)}) %collective-permute-start.17) | collective-permute-done | bytes 81952 | tf_op jit(solution)/shard_map/ppermute | solution.py:547
  71.6 3.3 %shard_map.135 = f32[16,32,256]{2,1,0:T(8,128)} custom-call(f32[32,640]{1,0:T(8,128)S(1)} %get-tuple-element.38.p0_ref, f32[32,640]{1,0:T(8,128)S(1)} %collective-permute-done.15.p1_ref, f32[32,640]{1,0:T(8,128)S(1)} %collective-permute-done.16.p2_ref, f32[32,640]{1,0:T(8,128)S(1)} %collective-permute-done.17.p3_ref, ...), custom_call_target="tpu_custom_call" | custom-call | flops 400000000 | bytes 1048576 | tf_op jit(solution)/shard_map/pallas_call | solution.py:479
  (45 shorter events, 0.3 us)
Async XLA Ops:
  0.0 1.0 %copy-start.7 = (f32[16,32,256]{2,1,0:T(8,128)S(1)}, f32[16,32,256]{2,1,0:T(8,128)}, u32[]{:S(2)}) copy-start(f32[16,32,256]{2,1,0:T(8,128)} %x_ref.9) | copy-start | bytes 1572868
  1.1 10.1 %collective-permute-start = (f32[16,3,256]{2,1,0:T(4,128)S(1)}, f32[16,3,256]{2,1,0:T(4,128)S(1)}, u32[]{:S(2)}, u32[]{:S(2)}) collective-permute-start(f32[16,3,256]{2,1,0:T(4,128)S(1)} %get-tuple-element.25), channel_id=1, source_target_pairs={{0,1},{1,0},{2,3},{3,2},{4,5},{5,4},{6,7},{7,6},{8,9},{9,8},{10,11... | collective-permute-start | bytes 147464 | tf_op jit(solution)/shard_map/ppermute | solution.py:495
  2.5 8.7 %collective-permute-start.1 = (f32[16,3,256]{2,1,0:T(4,128)S(1)}, f32[16,3,256]{2,1,0:T(4,128)S(1)}, u32[]{:S(2)}, u32[]{:S(2)}) collective-permute-start(f32[16,3,256]{2,1,0:T(4,128)S(1)} %get-tuple-element.26), channel_id=1, source_target_pairs={{1,2},{2,1},{3,4},{4,3},{5,6},{6,5},{7,8},{8,7},{9,10},{10,9},{11,... | collective-permute-start | bytes 147464 | tf_op jit(solution)/shard_map/ppermute | solution.py:496
  7.2 5.3 %copy-start.6 = (f32[256,768]{1,0:T(8,128)S(1)}, f32[256,768]{1,0:T(8,128)}, u32[]{:S(2)}) copy-start(f32[256,768]{1,0:T(8,128)} %wp_ref.3) | copy-start | bytes 2359300
  7.2 5.3 %copy-start.8 = (f32[256,256]{1,0:T(8,128)S(1)}, f32[256,256]{1,0:T(8,128)}, u32[]{:S(2)}) copy-start(f32[256,256]{1,0:T(8,128)} %wo_ref.3) | copy-start | bytes 786436
  7.2 5.3 %copy-start.10 = (f32[256]{0:T(256)S(1)}, f32[256]{0:T(256)}, u32[]{:S(2)}) copy-start(f32[256]{0:T(256)} %param.14) | copy-start | bytes 3076
  11.3 6.7 %collective-permute-start.2 = (f32[3,40,256]{2,1,0:T(8,128)S(1)}, f32[3,40,256]{2,1,0:T(8,128)S(1)}, u32[]{:S(2)}, u32[]{:S(2)}) collective-permute-start(f32[3,40,256]{2,1,0:T(8,128)S(1)} %get-tuple-element.27), channel_id=1, source_target_pairs={{0,16},{16,0},{1,17},{17,1},{2,18},{18,2},{3,19},{19,3},{4,20},{20... | collective-permute-start | bytes 368648 | tf_op jit(solution)/shard_map/ppermute | solution.py:507
  11.7 6.3 %collective-permute-start.3 = (f32[3,40,256]{2,1,0:T(8,128)S(1)}, f32[3,40,256]{2,1,0:T(8,128)S(1)}, u32[]{:S(2)}, u32[]{:S(2)}) collective-permute-start(f32[3,40,256]{2,1,0:T(8,128)S(1)} %get-tuple-element.28), channel_id=1, source_target_pairs={{16,32},{32,16},{48,64},{64,48},{80,96},{96,80},{17,33},{33,17},{4... | collective-permute-start | bytes 368648 | tf_op jit(solution)/shard_map/ppermute | solution.py:508
  12.5 5.4 %copy-start.2 = (f32[1536,512]{1,0:T(8,128)S(1)}, f32[1536,512]{1,0:T(8,128)}, u32[]{:S(2)}) copy-start(f32[1536,512]{1,0:T(8,128)} %m2_ref.1) | copy-start | bytes 9437188
  12.5 5.4 %copy-start.4 = (f32[1024,384]{1,0:T(8,128)S(1)}, f32[1024,384]{1,0:T(8,128)}, u32[]{:S(2)}) copy-start(f32[1024,384]{1,0:T(8,128)} %m1_ref.1) | copy-start | bytes 4718596
  12.6 5.4 %copy-start.9 = (f32[512]{0:T(512)S(1)}, f32[512]{0:T(512)}, u32[]{:S(2)}) copy-start(f32[512]{0:T(512)} %param.20) | copy-start | bytes 6148
  24.9 30.0 %copy-start.1 = (f32[512,1536]{1,0:T(8,128)S(1)}, f32[512,1536]{1,0:T(8,128)}, u32[]{:S(2)}) copy-start(f32[512,1536]{1,0:T(8,128)} %gp_ref.1) | copy-start | bytes 9437188
  27.8 6.7 %collective-permute-start.10 = (f32[32,512]{1,0:T(8,128)S(1)}, f32[32,512]{1,0:T(8,128)S(1)}, u32[]{:S(2)}, u32[]{:S(2)}) collective-permute-start(f32[32,512]{1,0:T(8,128)S(1)} %shard_map.132), channel_id=1, source_target_pairs={{0,1},{1,0},{2,3},{3,2},{4,5},{5,4},{6,7},{7,6},{8,9},{9,8},{10,11... | collective-permute-start | bytes 196616 | tf_op jit(solution)/shard_map/ppermute | solution.py:535
  27.9 11.0 %collective-permute-start.4 = (f32[32,512]{1,0:T(8,128)S(1)}, f32[32,512]{1,0:T(8,128)S(1)}, u32[]{:S(2)}, u32[]{:S(2)}) collective-permute-start(f32[32,512]{1,0:T(8,128)S(1)} %get-tuple-element.35.x_ref), channel_id=1, source_target_pairs={{0,2},{2,0},{16,18},{18,16},{1,3},{3,1},{17,19},{19,17},{4,6},{6,4... | collective-permute-start | bytes 196616 | tf_op jit(solution)/shard_map/ppermute | solution.py:452
  30.9 9.0 %collective-permute-start.5 = (f32[32,512]{1,0:T(8,128)S(1)}, f32[32,512]{1,0:T(8,128)S(1)}, u32[]{:S(2)}, u32[]{:S(2)}) collective-permute-start(f32[32,512]{1,0:T(8,128)S(1)} %get-tuple-element.35.x_ref), channel_id=1, source_target_pairs={{0,18},{2,16},{16,2},{18,0},{1,19},{3,17},{17,3},{19,1},{4,22},{6,... | collective-permute-start | bytes 196616 | tf_op jit(solution)/shard_map/ppermute | solution.py:452
  34.4 5.5 %collective-permute-start.6 = (f32[32,512]{1,0:T(8,128)S(1)}, f32[32,512]{1,0:T(8,128)S(1)}, u32[]{:S(2)}, u32[]{:S(2)}) collective-permute-start(f32[32,512]{1,0:T(8,128)S(1)} %get-tuple-element.35.x_ref), channel_id=1, source_target_pairs={{0,16},{2,18},{16,0},{18,2},{1,17},{3,19},{17,1},{19,3},{4,20},{6,... | collective-permute-start | bytes 196616 | tf_op jit(solution)/shard_map/ppermute | solution.py:452
  34.4 9.2 %collective-permute-start.11 = (f32[2,32,512]{2,1,0:T(8,128)S(1)}, f32[2,32,512]{2,1,0:T(8,128)S(1)}, u32[]{:S(2)}, u32[]{:S(2)}) collective-permute-start(f32[2,32,512]{2,1,0:T(8,128)S(1)} %pad_maximum_fusion), channel_id=1, source_target_pairs={{0,4},{4,0},{8,12},{12,8},{1,5},{5,1},{9,13},{13,9},{2,6},{6,2},{1... | collective-permute-start | bytes 393224 | tf_op jit(solution)/shard_map/ppermute | solution.py:452
  37.0 7.4 %collective-permute-start.12 = (f32[2,32,512]{2,1,0:T(8,128)S(1)}, f32[2,32,512]{2,1,0:T(8,128)S(1)}, u32[]{:S(2)}, u32[]{:S(2)}) collective-permute-start(f32[2,32,512]{2,1,0:T(8,128)S(1)} %pad_maximum_fusion), channel_id=1, source_target_pairs={{0,12},{4,8},{8,4},{12,0},{1,13},{5,9},{9,5},{13,1},{2,14},{6,10},... | collective-permute-start | bytes 393224 | tf_op jit(solution)/shard_map/ppermute | solution.py:452
  38.9 7.0 %collective-permute-start.13 = (f32[2,32,512]{2,1,0:T(8,128)S(1)}, f32[2,32,512]{2,1,0:T(8,128)S(1)}, u32[]{:S(2)}, u32[]{:S(2)}) collective-permute-start(f32[2,32,512]{2,1,0:T(8,128)S(1)} %pad_maximum_fusion), channel_id=1, source_target_pairs={{0,8},{4,12},{8,0},{12,4},{1,9},{5,13},{9,1},{13,5},{2,10},{6,14},... | collective-permute-start | bytes 393224 | tf_op jit(solution)/shard_map/ppermute | solution.py:452
  39.9 7.1 %collective-permute-start.7 = (f32[128,512]{1,0:T(8,128)S(1)}, f32[128,512]{1,0:T(8,128)S(1)}, u32[]{:S(2)}, u32[]{:S(2)}) collective-permute-start(f32[128,512]{1,0:T(8,128)S(1)} %constant_dynamic-update-slice_fusion.x0_ref), channel_id=1, source_target_pairs={{0,32},{32,0},{64,96},{96,64},{1,33},{33,1},{65,97},{97,65},{2,34}... | collective-permute-start | bytes 786440 | tf_op jit(solution)/shard_map/ppermute | solution.py:452
  41.7 7.6 %collective-permute-start.8 = (f32[128,512]{1,0:T(8,128)S(1)}, f32[128,512]{1,0:T(8,128)S(1)}, u32[]{:S(2)}, u32[]{:S(2)}) collective-permute-start(f32[128,512]{1,0:T(8,128)S(1)} %constant_dynamic-update-slice_fusion.x0_ref), channel_id=1, source_target_pairs={{0,96},{32,64},{64,32},{96,0},{1,97},{33,65},{65,33},{97,1},{2,98}... | collective-permute-start | bytes 786440 | tf_op jit(solution)/shard_map/ppermute | solution.py:452
  43.6 11.3 %collective-permute-start.9 = (f32[128,512]{1,0:T(8,128)S(1)}, f32[128,512]{1,0:T(8,128)S(1)}, u32[]{:S(2)}, u32[]{:S(2)}) collective-permute-start(f32[128,512]{1,0:T(8,128)S(1)} %constant_dynamic-update-slice_fusion.x0_ref), channel_id=1, source_target_pairs={{0,64},{32,96},{64,0},{96,32},{1,65},{33,97},{65,1},{97,33},{2,66}... | collective-permute-start | bytes 786440 | tf_op jit(solution)/shard_map/ppermute | solution.py:452
  45.9 25.7 %copy-start = (f32[512,1536]{1,0:T(8,128)S(1)}, f32[512,1536]{1,0:T(8,128)}, u32[]{:S(2)}) copy-start(f32[512,1536]{1,0:T(8,128)} %s2_ref.1) | copy-start | bytes 9437188
  45.9 25.7 %copy-start.3 = (f32[384,1024]{1,0:T(8,128)S(1)}, f32[384,1024]{1,0:T(8,128)}, u32[]{:S(2)}) copy-start(f32[384,1024]{1,0:T(8,128)} %s1_ref.1) | copy-start | bytes 4718596
  45.9 25.6 %copy-start.5 = (f32[512,512]{1,0:T(8,128)S(1)}, f32[512,512]{1,0:T(8,128)}, u32[]{:S(2)}) copy-start(f32[512,512]{1,0:T(8,128)} %go_ref.1) | copy-start | bytes 3145732
  60.2 3.7 %collective-permute-start.14 = (f32[4,32,640]{2,1,0:T(8,128)S(1)}, f32[4,32,640]{2,1,0:T(8,128)S(1)}, u32[]{:S(2)}, u32[]{:S(2)}) collective-permute-start(f32[4,32,640]{2,1,0:T(8,128)S(1)} %get-tuple-element.37), channel_id=1, source_target_pairs={{0,1},{1,0},{2,3},{3,2},{4,5},{5,4},{6,7},{7,6},{8,9},{9,8},{10,11... | collective-permute-start | bytes 983048 | tf_op jit(solution)/shard_map/ppermute | solution.py:544
  64.5 3.7 %collective-permute-start.15 = (f32[32,640]{1,0:T(8,128)S(1)}, f32[32,640]{1,0:T(8,128)S(1)}, u32[]{:S(2)}, u32[]{:S(2)}) collective-permute-start(f32[32,640]{1,0:T(8,128)S(1)} %get-tuple-element.39), channel_id=1, source_target_pairs={{0,4},{4,0},{8,12},{12,8},{1,5},{5,1},{9,13},{13,9},{2,6},{6,2},{1... | collective-permute-start | bytes 245768 | tf_op jit(solution)/shard_map/ppermute | solution.py:547
  64.9 4.5 %collective-permute-start.16 = (f32[32,640]{1,0:T(8,128)S(1)}, f32[32,640]{1,0:T(8,128)S(1)}, u32[]{:S(2)}, u32[]{:S(2)}) collective-permute-start(f32[32,640]{1,0:T(8,128)S(1)} %get-tuple-element.40), channel_id=1, source_target_pairs={{0,12},{4,8},{8,4},{12,0},{1,13},{5,9},{9,5},{13,1},{2,14},{6,10},... | collective-permute-start | bytes 245768 | tf_op jit(solution)/shard_map/ppermute | solution.py:547
  66.8 4.8 %collective-permute-start.17 = (f32[32,640]{1,0:T(8,128)S(1)}, f32[32,640]{1,0:T(8,128)S(1)}, u32[]{:S(2)}, u32[]{:S(2)}) collective-permute-start(f32[32,640]{1,0:T(8,128)S(1)} %get-tuple-element.41), channel_id=1, source_target_pairs={{0,8},{4,12},{8,0},{12,4},{1,9},{5,13},{9,1},{13,5},{2,10},{6,14},... | collective-permute-start | bytes 245768 | tf_op jit(solution)/shard_map/ppermute | solution.py:547
